TPU v7x, 128 devices: a whole 4x4x4 slice. The times are simulated.
128 devices in a mesh: gx: 16 (over x_lo, z, core), gy: 8 (over y, x_hi).
Axes of the slice: x: 4 (x_hi: 2, x_lo: 2; x = x_hi * 2 + x_lo), y: 4, z: 4, core: 2. Of those that a mesh axis runs over, the one named last changes fastest.
Arguments:
- right_side: float32 [256, 256, 128], P('gx', 'gy'), may hold values from -6 to 6
- shift: float32 [256, 256, 128], P('gx', 'gy'), may hold values from 0.5 to 8
Outputs:
- solution_field: float32 [256, 256, 128], P('gx', 'gy')
- residual: float32 [256, 256, 128], P('gx', 'gy')
All inputs are finite; a program needn't handle non-finite values.
Results may differ from a plain program's by a relative error of at most 0.0003.
Values sent between devices are 32-bit elements; how exact they have to be, the bound alone decides.
No kernel may reach another device: no remote copies, remote signals or barrier semaphores. Data moves between devices by JAX's collectives and lax.ppermute only.
A program may use at most 128 MiB of HBM per device.

v0:
```python
import jax
import jax.numpy as jnp
from jax import lax
from jax.sharding import Mesh
from jax.sharding import PartitionSpec as P

ITERS = 3
LEVELS = 3
SWEEPS = 2
BOTTOM = 4
GX = ("gx_0", "gx_1", "gx_2")
GY = ("gy_0", "gy_1")
GX_GY = ("gx_0", "gx_1", "gx_2", "gy_0", "gy_1")


relaxation = 0.7
center_weight = 26.0


def with_halo(block, sides, width):
    for axis, dim in sides:
        count = lax.axis_size(axis)
        forward = [(i, i + 1) for i in range(count - 1)]
        backward = [(target, source) for source, target in forward]
        low = lax.ppermute(
            lax.slice_in_dim(block, block.shape[dim] - width, None, axis=dim), axis, forward
        )
        high = lax.ppermute(lax.slice_in_dim(block, 0, width, axis=dim), axis, backward)
        block = jnp.concatenate([low, block, high], axis=dim)
    return block


def one_axis_at_a_time(x, axes):
    for axis in axes:
        x = lax.psum(x, axis)
    return x


def neighbours(padded):
    total = padded[:, :, :-2] + padded[:, :, 1:-1] + padded[:, :, 2:]
    total = total[:, :-2] + total[:, 1:-1] + total[:, 2:]
    total = total[:-2] + total[1:-1] + total[2:]
    return total - padded[1:-1, 1:-1, 1:-1]


def coarsen(field):
    first, second, third = field.shape
    return field.reshape(first // 2, 2, second // 2, 2, third // 2, 2).mean(axis=(1, 3, 5))


def prolong(field):
    return jnp.repeat(jnp.repeat(jnp.repeat(field, 2, 0), 2, 1), 2, 2)


def level_diagonals(box_shift):
    result = []
    current = box_shift
    for level in range(LEVELS):
        result.append(center_weight + 4.0**level * current)
        if level + 1 < LEVELS:
            current = coarsen(current)
    return result


def sweep(guess, source, diag):
    return guess + relaxation * (source - (diag * guess - neighbours(jnp.pad(guess, 1)))) / diag


def vcycle(rhs, diags, level):
    diag = diags[level]
    source = 4.0**level * rhs
    count = BOTTOM if level == LEVELS - 1 else SWEEPS
    guess = relaxation * source / diag
    for turn in range(count - 1):
        guess = sweep(guess, source, diag)
    if level < LEVELS - 1:
        leftover = (source - (diag * guess - neighbours(jnp.pad(guess, 1)))) / 4.0**level
        guess = guess + prolong(vcycle(coarsen(leftover), diags, level + 1))
        for turn in range(SWEEPS):
            guess = sweep(guess, source, diag)
    return guess


def fold_band(padded, dim, width):
    length = padded.shape[dim]
    core = lax.slice_in_dim(padded, 2 * width, length - 2 * width, axis=dim)
    inner = core.shape[dim]
    lower = lax.slice_in_dim(padded, 0, width, axis=dim)
    upper = lax.slice_in_dim(padded, length - width, length, axis=dim)
    head = lax.slice_in_dim(core, 0, width, axis=dim) + lower
    middle = lax.slice_in_dim(core, width, inner - width, axis=dim)
    tail = lax.slice_in_dim(core, inner - width, inner, axis=dim) + upper
    return jnp.concatenate([head, middle, tail], axis=dim)


def on_device(right_side, shift):
    cells_x = right_side.shape[0]
    cells_y = right_side.shape[1]
    total_x = cells_x * lax.axis_size(GX)
    total_y = cells_y * lax.axis_size(GY)

    def extend(field):
        return with_halo(field, ((GX, 0), (GY, 1)), 2)

    shift_box = extend(shift)
    diags = level_diagonals(shift_box)
    rows = lax.axis_index(GX) * cells_x - 2 + jnp.arange(cells_x + 4, dtype=jnp.int32)
    cols = lax.axis_index(GY) * cells_y - 2 + jnp.arange(cells_y + 4, dtype=jnp.int32)
    row_ok = ((rows >= 0) & (rows < total_x)).astype(jnp.float32)
    col_ok = ((cols >= 0) & (cols < total_y)).astype(jnp.float32)
    grid_mask = row_ok[:, None, None] * col_ok[None, :, None]
    widths = ((1, 1), (1, 1), (0, 0))
    shift_grown = jnp.pad(shift_box, widths)

    def precondition_image(residual):
        local = vcycle(extend(residual), diags, 0) * grid_mask
        grown = jnp.pad(local, widths)
        image_local = (center_weight + shift_grown) * grown - neighbours(jnp.pad(grown, 1))
        stacked = jnp.stack([grown, image_local])
        returned = with_halo(stacked, ((GX, 1), (GY, 2)), 3)
        folded = fold_band(fold_band(returned, 1, 3), 2, 3)
        return (folded[0], folded[1])

    solution_field = jnp.zeros_like(right_side)
    residual = right_side

    def paired_sums(residual, precond, image):
        return (
            one_axis_at_a_time(jnp.sum(residual * precond), GX_GY),
            one_axis_at_a_time(jnp.sum(image * precond), GX_GY),
        )

    precond, image = precondition_image(residual)
    rz_now, product = paired_sums(residual, precond, image)
    alpha = rz_now / product
    direction, along = (precond, image)
    for step in range(ITERS):
        solution_field = solution_field + alpha * direction
        residual = residual - alpha * along
        if step + 1 < ITERS:
            precond, image = precondition_image(residual)
            rz_next, product = paired_sums(residual, precond, image)
            ratio = rz_next / rz_now
            alpha = rz_next / (product - ratio * rz_next / alpha)
            direction = precond + ratio * direction
            along = image + ratio * along
            rz_now = rz_next
    return (solution_field, residual)


def solution(mesh):
    split = Mesh(mesh.devices.reshape(2, 4, 2, 4, 2), ("gx_0", "gx_1", "gx_2", "gy_0", "gy_1"))
    in_specs = (P(GX, GY, None), P(GX, GY, None))
    out_specs = (P(GX, GY, None), P(GX, GY, None))
    return jax.shard_map(
        on_device, mesh=split, in_specs=in_specs, out_specs=out_specs, check_vma=False
    )
```

profile of v0, /device:TPU:42, one launch (start us, length us, event | category | flops | bytes accessed | tf_op | source)
XLA Modules:
  0.0 480.9 jit_solution(9280216936747103945)
XLA Ops:
  37.0 25.3 %reshape.131 = f32[10,2,18,2,64,2]{5,4,3,2,1,0:T(8,128)} reshape(f32[20,36,128]{2,1,0:T(8,128)S(1)} %fusion.95) | data formatting | bytes 737280 | tf_op jit(solution)/shard_map/reshape | solution.py:48
  62.3 25.2 %reshape.132 = f32[10,2,18,2,64,2]{5,4,3,2,1,0:T(8,128)} reshape(f32[20,36,128]{2,1,0:T(8,128)S(1)} %get-tuple-element.68) | data formatting | bytes 737280 | tf_op jit(solution)/shard_map/reshape | solution.py:48
  87.5 9.1 %reduce_sum.126 = f32[10,18,64]{2,1,0:T(8,128)S(1)} reduce(f32[10,2,18,2,64,2]{5,4,3,2,1,0:T(8,128)} %reshape.131, f32[]{:T(128)} %constant.67.clone.1), dimensions={1,3,5}, to_apply=%region_0.0 | reduce | flops 80640 | bytes 414724 | tf_op jit(solution)/shard_map/reduce_sum | solution.py:48
  96.6 9.1 %reduce_sum.127 = f32[10,18,64]{2,1,0:T(8,128)S(1)} reduce(f32[10,2,18,2,64,2]{5,4,3,2,1,0:T(8,128)} %reshape.132, f32[]{:T(128)} %constant.67.clone.1), dimensions={1,3,5}, to_apply=%region_1.0 | reduce | flops 80640 | bytes 414724 | tf_op jit(solution)/shard_map/reduce_sum | solution.py:48
  133.2 5.8 %collective-permute-start.10 = (f32[2,28,3,128]{3,0,2,1:T(2,128)S(1)}, f32[2,28,3,128]{3,0,2,1:T(2,128)S(1)}, u32[]{:S(2)}, u32[]{:S(2)}) collective-permute-start(f32[2,28,3,128]{3,0,2,1:T(2,128)S(1)} %get-tuple-element.48), channel_id=1, source_target_pairs={{0,1},{1,2},{2,3},{3,4},{4,5},{5,6},{6,7},{8,9},{9,10},{10,11},{11... | collective-permute-start | bytes 258056 | tf_op jit(solution)/shard_map/ppermute | solution.py:25
  142.3 4.9 %collective-permute-done.11 = f32[2,28,3,128]{3,0,2,1:T(2,128)S(1)} collective-permute-done((f32[2,28,3,128]{3,0,2,1:T(2,128)S(1)}, f32[2,28,3,128]{3,0,2,1:T(2,128)S(1)}, u32[]{:S(2)}, u32[]{:S(2)}) %collective-permute-start.11) | collective-permute-done | bytes 86048 | tf_op jit(solution)/shard_map/ppermute | solution.py:28
  151.4 5.6 %all-reduce.54 = (f32[]{:T(128)}, f32[]{:T(128)}) all-reduce(f32[]{:T(128)} %get-tuple-element.11, f32[]{:T(128)} %get-tuple-element.10), channel_id=1, replica_groups=mesh['gx_0'=2,'gx_1'=4,'gx_2'=2,'gy_0'=4,'gy_1'=2] {'gx_0'}, use_global_device_ids=true, to_apply=%region_5.6 | all-reduce | flops 2 | bytes 16 | tf_op jit(solution)/shard_map/psum | solution.py:35
  156.9 18.0 %all-reduce.45 = (f32[]{:T(128)}, f32[]{:T(128)}) all-reduce(f32[]{:T(128)} %get-tuple-element.40, f32[]{:T(128)} %get-tuple-element.41), channel_id=1, replica_groups=mesh['gx_0'=2,'gx_1'=4,'gx_2'=2,'gy_0'=4,'gy_1'=2] {'gx_1'}, use_global_device_ids=true, to_apply=%region_6.7 | all-reduce | flops 2 | bytes 16 | tf_op jit(solution)/shard_map/psum | solution.py:35
  178.0 9.0 %all-reduce.42 = (f32[]{:T(128)}, f32[]{:T(128)}) all-reduce(f32[]{:T(128)} %get-tuple-element.34, f32[]{:T(128)} %get-tuple-element.35), channel_id=1, replica_groups=mesh['gx_0'=2,'gx_1'=4,'gx_2'=2,'gy_0'=4,'gy_1'=2] {'gy_0'}, use_global_device_ids=true, to_apply=%region_8.9 | all-reduce | flops 2 | bytes 16 | tf_op jit(solution)/shard_map/psum | solution.py:35
  187.0 7.1 %all-reduce.48 = (f32[]{:T(128)}, f32[]{:T(128)}) all-reduce(f32[]{:T(128)} %get-tuple-element.16, f32[]{:T(128)} %get-tuple-element.17), channel_id=1, replica_groups=mesh['gx_0'=2,'gx_1'=4,'gx_2'=2,'gy_0'=4,'gy_1'=2] {'gy_1'}, use_global_device_ids=true, to_apply=%region_9.10 | all-reduce | flops 2 | bytes 16 | tf_op jit(solution)/shard_map/psum | solution.py:35
  205.8 5.0 %collective-permute-start.15 = (f32[20,2,128]{2,1,0:T(2,128)S(1)}, f32[20,2,128]{2,1,0:T(2,128)S(1)}, u32[]{:S(2)}, u32[]{:S(2)}) collective-permute-start(f32[20,2,128]{2,1,0:T(2,128)S(1)} %get-tuple-element.73), channel_id=1, source_target_pairs={{1,0},{2,1},{3,2},{4,3},{5,4},{6,5},{7,6},{9,8},{10,9},{11,10},{12... | collective-permute-start | bytes 61448 | tf_op jit(solution)/shard_map/ppermute | solution.py:28
  214.4 25.8 %reshape.140 = f32[10,2,18,2,64,2]{5,4,3,2,1,0:T(8,128)} reshape(f32[20,36,128]{2,1,0:T(8,128)S(1)} %fusion.74) | data formatting | bytes 737280 | tf_op jit(solution)/shard_map/reshape | solution.py:48
  240.2 9.1 %reduce_sum.132 = f32[10,18,64]{2,1,0:T(8,128)S(1)} reduce(f32[10,2,18,2,64,2]{5,4,3,2,1,0:T(8,128)} %reshape.140, f32[]{:T(128)} %constant.67.clone.1), dimensions={1,3,5}, to_apply=%region_16.17 | reduce | flops 80640 | bytes 414724 | tf_op jit(solution)/shard_map/reduce_sum | solution.py:48
  290.2 5.6 %all-reduce.53 = (f32[]{:T(128)}, f32[]{:T(128)}) all-reduce(f32[]{:T(128)} %get-tuple-element.9, f32[]{:T(128)} %get-tuple-element.8), channel_id=1, replica_groups=mesh['gx_0'=2,'gx_1'=4,'gx_2'=2,'gy_0'=4,'gy_1'=2] {'gx_0'}, use_global_device_ids=true, to_apply=%region_19.20 | all-reduce | flops 2 | bytes 16 | tf_op jit(solution)/shard_map/psum | solution.py:35
  295.8 12.6 %all-reduce.44 = (f32[]{:T(128)}, f32[]{:T(128)}) all-reduce(f32[]{:T(128)} %get-tuple-element.38, f32[]{:T(128)} %get-tuple-element.39), channel_id=1, replica_groups=mesh['gx_0'=2,'gx_1'=4,'gx_2'=2,'gy_0'=4,'gy_1'=2] {'gx_1'}, use_global_device_ids=true, to_apply=%region_20.21 | all-reduce | flops 2 | bytes 16 | tf_op jit(solution)/shard_map/psum | solution.py:35
  311.4 10.2 %all-reduce.41 = (f32[]{:T(128)}, f32[]{:T(128)}) all-reduce(f32[]{:T(128)} %get-tuple-element.32, f32[]{:T(128)} %get-tuple-element.33), channel_id=1, replica_groups=mesh['gx_0'=2,'gx_1'=4,'gx_2'=2,'gy_0'=4,'gy_1'=2] {'gy_0'}, use_global_device_ids=true, to_apply=%region_22.23 | all-reduce | flops 2 | bytes 16 | tf_op jit(solution)/shard_map/psum | solution.py:35
  321.6 7.0 %all-reduce.47 = (f32[]{:T(128)}, f32[]{:T(128)}) all-reduce(f32[]{:T(128)} %get-tuple-element.14, f32[]{:T(128)} %get-tuple-element.15), channel_id=1, replica_groups=mesh['gx_0'=2,'gx_1'=4,'gx_2'=2,'gy_0'=4,'gy_1'=2] {'gy_1'}, use_global_device_ids=true, to_apply=%region_23.24 | all-reduce | flops 2 | bytes 16 | tf_op jit(solution)/shard_map/psum | solution.py:35
  343.7 5.0 %collective-permute-start.23 = (f32[20,2,128]{2,1,0:T(2,128)S(1)}, f32[20,2,128]{2,1,0:T(2,128)S(1)}, u32[]{:S(2)}, u32[]{:S(2)}) collective-permute-start(f32[20,2,128]{2,1,0:T(2,128)S(1)} %get-tuple-element.71), channel_id=1, source_target_pairs={{1,0},{2,1},{3,2},{4,3},{5,4},{6,5},{7,6},{9,8},{10,9},{11,10},{12... | collective-permute-start | bytes 61448 | tf_op jit(solution)/shard_map/ppermute | solution.py:28
  353.0 26.0 %reshape.148 = f32[10,2,18,2,64,2]{5,4,3,2,1,0:T(8,128)} reshape(f32[20,36,128]{2,1,0:T(8,128)} %fusion.53) | data formatting | bytes 737280 | tf_op jit(solution)/shard_map/reshape | solution.py:48
  379.0 9.1 %reduce_sum.136 = f32[10,18,64]{2,1,0:T(8,128)S(1)} reduce(f32[10,2,18,2,64,2]{5,4,3,2,1,0:T(8,128)} %reshape.148, f32[]{:T(128)} %constant.67.clone.1), dimensions={1,3,5}, to_apply=%region_30.31 | reduce | flops 80640 | bytes 414724 | tf_op jit(solution)/shard_map/reduce_sum | solution.py:48
  436.3 5.6 %all-reduce.52 = (f32[]{:T(128)}, f32[]{:T(128)}) all-reduce(f32[]{:T(128)} %get-tuple-element.7, f32[]{:T(128)} %get-tuple-element.6), channel_id=1, replica_groups=mesh['gx_0'=2,'gx_1'=4,'gx_2'=2,'gy_0'=4,'gy_1'=2] {'gx_0'}, use_global_device_ids=true, to_apply=%region_33.34 | all-reduce | flops 2 | bytes 16 | tf_op jit(solution)/shard_map/psum | solution.py:35
  441.9 12.6 %all-reduce.43 = (f32[]{:T(128)}, f32[]{:T(128)}) all-reduce(f32[]{:T(128)} %get-tuple-element.36, f32[]{:T(128)} %get-tuple-element.37), channel_id=1, replica_groups=mesh['gx_0'=2,'gx_1'=4,'gx_2'=2,'gy_0'=4,'gy_1'=2] {'gx_1'}, use_global_device_ids=true, to_apply=%region_34.35 | all-reduce | flops 2 | bytes 16 | tf_op jit(solution)/shard_map/psum | solution.py:35
  457.6 11.2 %all-reduce.40 = (f32[]{:T(128)}, f32[]{:T(128)}) all-reduce(f32[]{:T(128)} %get-tuple-element.30, f32[]{:T(128)} %get-tuple-element.31), channel_id=1, replica_groups=mesh['gx_0'=2,'gx_1'=4,'gx_2'=2,'gy_0'=4,'gy_1'=2] {'gy_0'}, use_global_device_ids=true, to_apply=%region_36.37 | all-reduce | flops 2 | bytes 16 | tf_op jit(solution)/shard_map/psum | solution.py:35
  468.8 7.1 %all-reduce.46 = (f32[]{:T(128)}, f32[]{:T(128)}) all-reduce(f32[]{:T(128)} %get-tuple-element.12, f32[]{:T(128)} %get-tuple-element.13), channel_id=1, replica_groups=mesh['gx_0'=2,'gx_1'=4,'gx_2'=2,'gy_0'=4,'gy_1'=2] {'gy_1'}, use_global_device_ids=true, to_apply=%region_37.38 | all-reduce | flops 2 | bytes 16 | tf_op jit(solution)/shard_map/psum | solution.py:35
  (344 shorter events, 197.6 us)
Async XLA Ops:
  1.5 23.1 %collective-permute-start.5 = (f32[2,32,128]{2,1,0:T(8,128)S(1)}, f32[2,32,128]{2,1,0:T(8,128)S(1)}, u32[]{:S(2)}, u32[]{:S(2)}) collective-permute-start(f32[2,32,128]{2,1,0:T(8,128)S(1)} %get-tuple-element.82), channel_id=1, source_target_pairs={{8,0},{16,8},{24,16},{32,24},{40,32},{48,40},{56,48},{64,56},{72,6... | collective-permute-start | bytes 98312 | tf_op jit(solution)/shard_map/ppermute | solution.py:28
  3.4 21.1 %collective-permute-start.4 = (f32[2,32,128]{2,1,0:T(8,128)S(1)}, f32[2,32,128]{2,1,0:T(8,128)S(1)}, u32[]{:S(2)}, u32[]{:S(2)}) collective-permute-start(f32[2,32,128]{2,1,0:T(8,128)S(1)} %get-tuple-element.83), channel_id=1, source_target_pairs={{0,8},{8,16},{16,24},{24,32},{32,40},{40,48},{48,56},{56,64},{64,7... | collective-permute-start | bytes 98312 | tf_op jit(solution)/shard_map/ppermute | solution.py:25
  6.6 9.6 %collective-permute-start.1 = (f32[2,32,128]{2,1,0:T(8,128)S(1)}, f32[2,32,128]{2,1,0:T(8,128)S(1)}, u32[]{:S(2)}, u32[]{:S(2)}) collective-permute-start(f32[2,32,128]{2,1,0:T(8,128)S(1)} %get-tuple-element.84), channel_id=1, source_target_pairs={{8,0},{16,8},{24,16},{32,24},{40,32},{48,40},{56,48},{64,56},{72,6... | collective-permute-start | bytes 98312 | tf_op jit(solution)/shard_map/ppermute | solution.py:28
  16.2 16.7 %collective-permute-start.2 = (f32[20,2,128]{2,1,0:T(2,128)S(1)}, f32[20,2,128]{2,1,0:T(2,128)S(1)}, u32[]{:S(2)}, u32[]{:S(2)}) collective-permute-start(f32[20,2,128]{2,1,0:T(2,128)S(1)} %get-tuple-element.76), channel_id=1, source_target_pairs={{0,1},{1,2},{2,3},{3,4},{4,5},{5,6},{6,7},{8,9},{9,10},{10,11},{11... | collective-permute-start | bytes 61448 | tf_op jit(solution)/shard_map/ppermute | solution.py:25
  20.5 12.4 %collective-permute-start.3 = (f32[20,2,128]{2,1,0:T(2,128)S(1)}, f32[20,2,128]{2,1,0:T(2,128)S(1)}, u32[]{:S(2)}, u32[]{:S(2)}) collective-permute-start(f32[20,2,128]{2,1,0:T(2,128)S(1)} %get-tuple-element.77), channel_id=1, source_target_pairs={{1,0},{2,1},{3,2},{4,3},{5,4},{6,5},{7,6},{9,8},{10,9},{11,10},{12... | collective-permute-start | bytes 61448 | tf_op jit(solution)/shard_map/ppermute | solution.py:28
  24.6 8.4 %collective-permute-start.6 = (f32[20,2,128]{2,1,0:T(2,128)S(1)}, f32[20,2,128]{2,1,0:T(2,128)S(1)}, u32[]{:S(2)}, u32[]{:S(2)}) collective-permute-start(f32[20,2,128]{2,1,0:T(2,128)S(1)} %get-tuple-element.74), channel_id=1, source_target_pairs={{0,1},{1,2},{2,3},{3,4},{4,5},{5,6},{6,7},{8,9},{9,10},{10,11},{11... | collective-permute-start | bytes 61448 | tf_op jit(solution)/shard_map/ppermute | solution.py:25
  28.0 7.2 %collective-permute-start.7 = (f32[20,2,128]{2,1,0:T(2,128)S(1)}, f32[20,2,128]{2,1,0:T(2,128)S(1)}, u32[]{:S(2)}, u32[]{:S(2)}) collective-permute-start(f32[20,2,128]{2,1,0:T(2,128)S(1)} %get-tuple-element.75), channel_id=1, source_target_pairs={{1,0},{2,1},{3,2},{4,3},{5,4},{6,5},{7,6},{9,8},{10,9},{11,10},{12... | collective-permute-start | bytes 61448 | tf_op jit(solution)/shard_map/ppermute | solution.py:28
  125.1 6.1 %collective-permute-start.8 = (f32[2,3,38,128]{3,0,2,1:T(2,128)S(1)}, f32[2,3,38,128]{3,0,2,1:T(2,128)S(1)}, u32[]{:S(2)}, u32[]{:S(2)}) collective-permute-start(f32[2,3,38,128]{3,0,2,1:T(2,128)S(1)} %get-tuple-element.60), channel_id=1, source_target_pairs={{0,8},{8,16},{16,24},{24,32},{32,40},{40,48},{48,56},{56,64},{64,7... | collective-permute-start | bytes 350216 | tf_op jit(solution)/shard_map/ppermute | solution.py:25
  127.1 6.0 %collective-permute-start.9 = (f32[2,3,38,128]{3,0,2,1:T(2,128)S(1)}, f32[2,3,38,128]{3,0,2,1:T(2,128)S(1)}, u32[]{:S(2)}, u32[]{:S(2)}) collective-permute-start(f32[2,3,38,128]{3,0,2,1:T(2,128)S(1)} %get-tuple-element.61), channel_id=1, source_target_pairs={{8,0},{16,8},{24,16},{32,24},{40,32},{48,40},{56,48},{64,56},{72,6... | collective-permute-start | bytes 350216 | tf_op jit(solution)/shard_map/ppermute | solution.py:28
  133.2 9.0 %collective-permute-start.10 = (f32[2,28,3,128]{3,0,2,1:T(2,128)S(1)}, f32[2,28,3,128]{3,0,2,1:T(2,128)S(1)}, u32[]{:S(2)}, u32[]{:S(2)}) collective-permute-start(f32[2,28,3,128]{3,0,2,1:T(2,128)S(1)} %get-tuple-element.48), channel_id=1, source_target_pairs={{0,1},{1,2},{2,3},{3,4},{4,5},{5,6},{6,7},{8,9},{9,10},{10,11},{11... | collective-permute-start | bytes 258056 | tf_op jit(solution)/shard_map/ppermute | solution.py:25
  139.1 8.1 %collective-permute-start.11 = (f32[2,28,3,128]{3,0,2,1:T(2,128)S(1)}, f32[2,28,3,128]{3,0,2,1:T(2,128)S(1)}, u32[]{:S(2)}, u32[]{:S(2)}) collective-permute-start(f32[2,28,3,128]{3,0,2,1:T(2,128)S(1)} %get-tuple-element.49), channel_id=1, source_target_pairs={{1,0},{2,1},{3,2},{4,3},{5,4},{6,5},{7,6},{9,8},{10,9},{11,10},{12... | collective-permute-start | bytes 258056 | tf_op jit(solution)/shard_map/ppermute | solution.py:28
  195.4 5.6 %collective-permute-start.12 = (f32[2,32,128]{2,1,0:T(8,128)S(1)}, f32[2,32,128]{2,1,0:T(8,128)S(1)}, u32[]{:S(2)}, u32[]{:S(2)}) collective-permute-start(f32[2,32,128]{2,1,0:T(8,128)S(1)} %get-tuple-element.80), channel_id=1, source_target_pairs={{0,8},{8,16},{16,24},{24,32},{32,40},{40,48},{48,56},{56,64},{64,7... | collective-permute-start | bytes 98312 | tf_op jit(solution)/shard_map/ppermute | solution.py:25
  202.5 8.3 %collective-permute-start.14 = (f32[20,2,128]{2,1,0:T(2,128)S(1)}, f32[20,2,128]{2,1,0:T(2,128)S(1)}, u32[]{:S(2)}, u32[]{:S(2)}) collective-permute-start(f32[20,2,128]{2,1,0:T(2,128)S(1)} %get-tuple-element.72), channel_id=1, source_target_pairs={{0,1},{1,2},{2,3},{3,4},{4,5},{5,6},{6,7},{8,9},{9,10},{10,11},{11... | collective-permute-start | bytes 61448 | tf_op jit(solution)/shard_map/ppermute | solution.py:25
  205.8 7.2 %collective-permute-start.15 = (f32[20,2,128]{2,1,0:T(2,128)S(1)}, f32[20,2,128]{2,1,0:T(2,128)S(1)}, u32[]{:S(2)}, u32[]{:S(2)}) collective-permute-start(f32[20,2,128]{2,1,0:T(2,128)S(1)} %get-tuple-element.73), channel_id=1, source_target_pairs={{1,0},{2,1},{3,2},{4,3},{5,4},{6,5},{7,6},{9,8},{10,9},{11,10},{12... | collective-permute-start | bytes 61448 | tf_op jit(solution)/shard_map/ppermute | solution.py:28
  265.9 6.1 %collective-permute-start.16 = (f32[2,3,38,128]{3,0,2,1:T(2,128)S(1)}, f32[2,3,38,128]{3,0,2,1:T(2,128)S(1)}, u32[]{:S(2)}, u32[]{:S(2)}) collective-permute-start(f32[2,3,38,128]{3,0,2,1:T(2,128)S(1)} %get-tuple-element.58), channel_id=1, source_target_pairs={{0,8},{8,16},{16,24},{24,32},{32,40},{40,48},{48,56},{56,64},{64,7... | collective-permute-start | bytes 350216 | tf_op jit(solution)/shard_map/ppermute | solution.py:25
  267.8 6.0 %collective-permute-start.17 = (f32[2,3,38,128]{3,0,2,1:T(2,128)S(1)}, f32[2,3,38,128]{3,0,2,1:T(2,128)S(1)}, u32[]{:S(2)}, u32[]{:S(2)}) collective-permute-start(f32[2,3,38,128]{3,0,2,1:T(2,128)S(1)} %get-tuple-element.59), channel_id=1, source_target_pairs={{8,0},{16,8},{24,16},{32,24},{40,32},{48,40},{56,48},{64,56},{72,6... | collective-permute-start | bytes 350216 | tf_op jit(solution)/shard_map/ppermute | solution.py:28
  274.0 8.8 %collective-permute-start.18 = (f32[2,28,3,128]{3,0,2,1:T(2,128)S(1)}, f32[2,28,3,128]{3,0,2,1:T(2,128)S(1)}, u32[]{:S(2)}, u32[]{:S(2)}) collective-permute-start(f32[2,28,3,128]{3,0,2,1:T(2,128)S(1)} %get-tuple-element.46), channel_id=1, source_target_pairs={{0,1},{1,2},{2,3},{3,4},{4,5},{5,6},{6,7},{8,9},{9,10},{10,11},{11... | collective-permute-start | bytes 258056 | tf_op jit(solution)/shard_map/ppermute | solution.py:25
  278.6 7.9 %collective-permute-start.19 = (f32[2,28,3,128]{3,0,2,1:T(2,128)S(1)}, f32[2,28,3,128]{3,0,2,1:T(2,128)S(1)}, u32[]{:S(2)}, u32[]{:S(2)}) collective-permute-start(f32[2,28,3,128]{3,0,2,1:T(2,128)S(1)} %get-tuple-element.47), channel_id=1, source_target_pairs={{1,0},{2,1},{3,2},{4,3},{5,4},{6,5},{7,6},{9,8},{10,9},{11,10},{12... | collective-permute-start | bytes 258056 | tf_op jit(solution)/shard_map/ppermute | solution.py:28
  340.4 8.3 %collective-permute-start.22 = (f32[20,2,128]{2,1,0:T(2,128)S(1)}, f32[20,2,128]{2,1,0:T(2,128)S(1)}, u32[]{:S(2)}, u32[]{:S(2)}) collective-permute-start(f32[20,2,128]{2,1,0:T(2,128)S(1)} %get-tuple-element.70), channel_id=1, source_target_pairs={{0,1},{1,2},{2,3},{3,4},{4,5},{5,6},{6,7},{8,9},{9,10},{10,11},{11... | collective-permute-start | bytes 61448 | tf_op jit(solution)/shard_map/ppermute | solution.py:25
  343.7 7.2 %collective-permute-start.23 = (f32[20,2,128]{2,1,0:T(2,128)S(1)}, f32[20,2,128]{2,1,0:T(2,128)S(1)}, u32[]{:S(2)}, u32[]{:S(2)}) collective-permute-start(f32[20,2,128]{2,1,0:T(2,128)S(1)} %get-tuple-element.71), channel_id=1, source_target_pairs={{1,0},{2,1},{3,2},{4,3},{5,4},{6,5},{7,6},{9,8},{10,9},{11,10},{12... | collective-permute-start | bytes 61448 | tf_op jit(solution)/shard_map/ppermute | solution.py:28
  412.9 6.1 %collective-permute-start.24 = (f32[2,3,38,128]{3,0,2,1:T(2,128)S(1)}, f32[2,3,38,128]{3,0,2,1:T(2,128)S(1)}, u32[]{:S(2)}, u32[]{:S(2)}) collective-permute-start(f32[2,3,38,128]{3,0,2,1:T(2,128)S(1)} %get-tuple-element.56), channel_id=1, source_target_pairs={{0,8},{8,16},{16,24},{24,32},{32,40},{40,48},{48,56},{56,64},{64,7... | collective-permute-start | bytes 350216 | tf_op jit(solution)/shard_map/ppermute | solution.py:25
  414.9 6.0 %collective-permute-start.25 = (f32[2,3,38,128]{3,0,2,1:T(2,128)S(1)}, f32[2,3,38,128]{3,0,2,1:T(2,128)S(1)}, u32[]{:S(2)}, u32[]{:S(2)}) collective-permute-start(f32[2,3,38,128]{3,0,2,1:T(2,128)S(1)} %get-tuple-element.57), channel_id=1, source_target_pairs={{8,0},{16,8},{24,16},{32,24},{40,32},{48,40},{56,48},{64,56},{72,6... | collective-permute-start | bytes 350216 | tf_op jit(solution)/shard_map/ppermute | solution.py:28
  421.0 8.8 %collective-permute-start.26 = (f32[2,28,3,128]{3,0,2,1:T(2,128)S(1)}, f32[2,28,3,128]{3,0,2,1:T(2,128)S(1)}, u32[]{:S(2)}, u32[]{:S(2)}) collective-permute-start(f32[2,28,3,128]{3,0,2,1:T(2,128)S(1)} %get-tuple-element.44), channel_id=1, source_target_pairs={{0,1},{1,2},{2,3},{3,4},{4,5},{5,6},{6,7},{8,9},{9,10},{10,11},{11... | collective-permute-start | bytes 258056 | tf_op jit(solution)/shard_map/ppermute | solution.py:25
  424.6 7.9 %collective-permute-start.27 = (f32[2,28,3,128]{3,0,2,1:T(2,128)S(1)}, f32[2,28,3,128]{3,0,2,1:T(2,128)S(1)}, u32[]{:S(2)}, u32[]{:S(2)}) collective-permute-start(f32[2,28,3,128]{3,0,2,1:T(2,128)S(1)} %get-tuple-element.45), channel_id=1, source_target_pairs={{1,0},{2,1},{3,2},{4,3},{5,4},{6,5},{7,6},{9,8},{10,9},{11,10},{12... | collective-permute-start | bytes 258056 | tf_op jit(solution)/shard_map/ppermute | solution.py:28
  (25 other events, 211.5 us)
where the time goes:
time: 490 us; the launch traced here: 481 us
  local copies, waits for them, and re-layouts  149 us (30%)
  blocking collectives  121 us (25%)
  starting transfers between devices  95.2 us (19%)
  other arithmetic  70.7 us (14%)
  waiting for transfers between devices  33.1 us (7%)
  between operations  12.4 us (3%)
    psum x15, blocking collectives, one_axis_at_a_time(): x = lax.psum(x, axis)  121 us
    reshape x7, local copies, waits for them, and re-layouts, coarsen(): field.reshape(first // 2, 2, second // 2, 2, third // 2, 2)  116 us
    ppermute x14, starting transfers between devices, with_halo(): lax.ppermute(lax.slice_in_dim(block, 0, width, axis=dim), axis, backward)  52.7 us
    ppermute x14, starting transfers between devices, with_halo(): lax.ppermute(lax.slice_in_dim(block, block.shape[dim] - width, None, axis...  42.5 us
    reduce_sum x8, other arithmetic, coarsen(): field.reshape(first // 2, 2, second // 2, 2, third // 2, 2)  41.2 us
    ppermute x14, waiting for transfers between devices, with_halo(): lax.ppermute(lax.slice_in_dim(block, 0, width, axis=dim), axis, backward)  26.4 us
    reshape x18, local copies, waits for them, and re-layouts, prolong(): return jnp.repeat(jnp.repeat(jnp.repeat(field, 2, 0), 2, 1), 2, 2)  10.5 us
  transfers between devices with their start and end apart: 28, of which 18 were waited for; matrix products, arithmetic and copies ran while one was open for 0% of the time, Pallas kernels for 0%

commit v1 on v0

v1 whole, which is shorter than its diff:
```python
import jax
import jax.numpy as jnp
from jax import lax
from jax.experimental import pallas as pl
from jax.experimental.pallas import tpu as pltpu
from jax.sharding import PartitionSpec as P

STEP = 0.5
RELAX = 0.7
CENTER = 26.0
AX = ("gx", "gy")
CX, CY, CZ = 16, 32, 128
ROWS = 40
BX = CX + 4
WX = CX + 6
F32 = jnp.float32
YBAND = 5
YROWS = 112
IROWS = 80


def sds(*shape):
    return jax.ShapeDtypeStruct(shape, F32)


def lanes():
    return lax.broadcasted_iota(jnp.int32, (ROWS, CZ), 1)


def rows():
    return lax.broadcasted_iota(jnp.int32, (ROWS, CZ), 0)


def zy_sum(p, sh):
    lane = lanes()
    zs = p + jnp.where(lane >= sh, pltpu.roll(p, sh, 1), 0.0)
    zs = zs + jnp.where(lane < CZ - sh, pltpu.roll(p, CZ - sh, 1), 0.0)
    return zs + pltpu.roll(zs, sh, 0) + pltpu.roll(zs, ROWS - sh, 0)


def stencil(n, sh, load, emit):
    prev = None
    cur = zy_sum(load(0), sh)
    for x in range(n):
        nxt = zy_sum(load(x + 1), sh) if x + 1 < n else None
        total = cur
        if prev is not None:
            total = total + prev
        if nxt is not None:
            total = total + nxt
        emit(x, total)
        prev, cur = cur, nxt


def pair_sum(a, level):
    sh = 2**level
    bit = ((rows() + 7) >> level) & 1
    a = a + jnp.where(bit == 0, pltpu.roll(a, ROWS - sh, 0), pltpu.roll(a, sh, 0))
    bit = (lanes() >> level) & 1
    return a + jnp.where(bit == 0, pltpu.roll(a, CZ - sh, 1), pltpu.roll(a, sh, 1))


def smooth(n, sh, e, g, w):
    def emit(x, total):
        here = e[x]
        e[x] = (1.0 - RELAX) * here + w[x] * (g[x] + (total - here))

    stencil(n, sh, lambda x: e[x], emit)


def restrict(n, level, e, g, dp1, g_next):
    held = []

    def emit(x, total):
        left = (g[x] + total) - dp1[x] * e[x]
        if x % 2 == 0:
            held.append(left)
        else:
            g_next[x // 2] = 0.5 * pair_sum(held.pop() + left, level)

    stencil(n, 2**level, lambda x: e[x], emit)


def vcycle(e0, g0, dp1_0, w0, dp1_1, w1, w2, e1, g1, e2, g2):
    n0, n1, n2 = BX, BX // 2, BX // 4
    for x in range(n0):
        e0[x] = w0[x] * g0[x]
    smooth(n0, 1, e0, g0, w0)
    restrict(n0, 0, e0, g0, dp1_0, g1)
    for x in range(n1):
        e1[x] = w1[x] * g1[x]
    smooth(n1, 2, e1, g1, w1)
    restrict(n1, 1, e1, g1, dp1_1, g2)
    for x in range(n2):
        e2[x] = w2[x] * g2[x]
    for _ in range(3):
        smooth(n2, 4, e2, g2, w2)
    for x in range(n1):
        e1[x] = e1[x] + e2[x // 2]
    for _ in range(2):
        smooth(n1, 2, e1, g1, w1)
    for x in range(n0):
        e0[x] = e0[x] + e1[x // 2]
    for _ in range(2):
        smooth(n0, 1, e0, g0, w0)


def send_x(idx, v, out_a, out_b):
    low, high = 1, CX
    a = jnp.where(idx[0] == 0, high, low)
    b = jnp.where(idx[0] == 0, low, high)
    out_a[...] = v[pl.ds(a, YBAND)]
    out_b[...] = v[pl.ds(b, YBAND)]


def add_x(idx, w, in_a, in_b):
    low, high = 0, CX + 1
    a = jnp.where(idx[0] == 0, high, low)
    b = jnp.where(idx[0] == 0, low, high)
    w[pl.ds(a, YBAND)] = w[pl.ds(a, YBAND)] + in_a[...]
    w[pl.ds(b, YBAND)] = w[pl.ds(b, YBAND)] + in_b[...]


def pack_x_kernel(idx, r, s, out_a, out_b):
    a = jnp.where(idx[0] == 0, CX - 2, 0)
    b = jnp.where(idx[0] == 0, 0, CX - 2)
    out_a[0] = r[pl.ds(a, 2)]
    out_a[1] = s[pl.ds(a, 2)]
    out_b[0] = r[pl.ds(b, 2)]
    out_b[1] = s[pl.ds(b, 2)]


def box_kernel(idx, r, s, in_a, in_b, rbox, sbox, out_a, out_b, pack):
    even = idx[0] == 0
    a = jnp.where(even, CX + 2, 0)
    b = jnp.where(even, 0, CX + 2)
    for k, (src, dst) in enumerate(((r, rbox), (s, sbox))):
        dst[...] = jnp.zeros_like(dst)
        for x in range(CX):
            dst[x + 2, 3 : 3 + CY, :] = src[x]
        for x in range(2):
            dst[a + x, 3 : 3 + CY, :] = in_a[k, x]
            dst[b + x, 3 : 3 + CY, :] = in_b[k, x]
        for x in range(BX):
            pack[0, 4 * x + 2 * k : 4 * x + 2 * k + 2, :] = dst[x, 3:5, :]
            pack[1, 4 * x + 2 * k : 4 * x + 2 * k + 2, :] = dst[x, 33:35, :]
    up = jnp.where(idx[1] == 0, 1, 0)
    out_a[...] = pack[up]
    out_b[...] = pack[1 - up]


def first_kernel(
    idx, rin, sin, in_a, in_b,
    r0, v, out_a, out_b, dp1_0, w0, dp1_1, w1, w2,
    got, s0, s1, e1, g1, e2, g2,
):
    up = jnp.where(idx[1] == 0, 1, 0)
    got[up] = in_a[...]
    got[1 - up] = in_b[...]
    row = rows()
    inside = (row >= 1) & (row < 37)
    for k, (src, dst) in enumerate(((rin, r0), (sin, s0))):
        dst[...] = src[...]
        for x in range(BX):
            dst[x, 1:3, :] = got[0, 4 * x + 2 * k : 4 * x + 2 * k + 2, :]
            dst[x, 35:37, :] = got[1, 4 * x + 2 * k : 4 * x + 2 * k + 2, :]

    def coefficients(n, scale, s, dp1, w):
        for x in range(n):
            d = CENTER + scale * s[x]
            if dp1 is not None:
                dp1[x] = d + 1.0
            w[x] = jnp.where(inside, RELAX / d, 0.0)

    coefficients(BX, 1.0, s0, dp1_0, w0)
    for x in range(BX // 2):
        s1[x] = 0.125 * pair_sum(s0[2 * x] + s0[2 * x + 1], 0)
    coefficients(BX // 2, 4.0, s1, dp1_1, w1)
    for x in range(BX // 4):
        s0[x] = 0.125 * pair_sum(s1[2 * x] + s1[2 * x + 1], 1)
    coefficients(BX // 4, 16.0, s0, None, w2)
    v[0] = jnp.zeros((ROWS, CZ), F32)
    v[WX - 1] = jnp.zeros((ROWS, CZ), F32)
    vcycle(v.at[pl.ds(1, BX)], r0, dp1_0, w0, dp1_1, w1, w2, e1, g1, e2, g2)
    send_x(idx, v, out_a, out_b)


def pack_y_kernel(idx, v, in_a, in_b, out_a, out_b, w, pack):
    for x in range(WX):
        w[x, 0:8, :] = v[x, 0:8, :]
        w[x, 8:16, :] = v[x, 32:40, :]
    a = jnp.where(idx[0] == 0, CX + 1, 0)
    b = jnp.where(idx[0] == 0, 0, CX + 1)
    for first, src in ((a, in_a), (b, in_b)):
        for x in range(YBAND):
            w[first + x, 0:8, :] = w[first + x, 0:8, :] + src[x, 0:8, :]
            w[first + x, 8:16, :] = w[first + x, 8:16, :] + src[x, 32:40, :]
    pack[:, YROWS - 8 :, :] = jnp.zeros((2, 8, CZ), F32)
    for x in range(WX):
        pack[0, YBAND * x : YBAND * x + YBAND, :] = w[x, 1:6, :]
        pack[1, YBAND * x : YBAND * x + YBAND, :] = w[x, 8:13, :]
    up = jnp.where(idx[1] == 0, 1, 0)
    out_a[...] = pack[up]
    out_b[...] = pack[1 - up]


def assemble(idx, w, v, xa, xb, ya, yb, got):
    w[...] = v[...]
    add_x(idx, w, xa, xb)
    up = jnp.where(idx[1] == 0, 1, 0)
    got[up] = ya[...]
    got[1 - up] = yb[...]
    row = rows()
    mask = jnp.where(((row >= 3) | (idx[4] == 0)) & ((row < 3 + CY) | (idx[5] == 0)), 1.0, 0.0)
    for x in range(WX):
        w[x, 0:5, :] = w[x, 0:5, :] + got[0, YBAND * x : YBAND * x + YBAND, :]
        w[x, 33:38, :] = w[x, 33:38, :] + got[1, YBAND * x : YBAND * x + YBAND, :]
        m = mask
        if x < 3:
            m = mask * jnp.where(idx[2] == 0, 1.0, 0.0)
        if x >= CX + 3:
            m = mask * jnp.where(idx[3] == 0, 1.0, 0.0)
        w[x] = w[x] * m


def box_mask(idx, x):
    row = rows()
    low = jnp.where(idx[4] == 0, 1, 3)
    high = jnp.where(idx[5] == 0, 37, 35)
    m = jnp.where((row >= low) & (row < high), 1.0, 0.0)
    if x < 2:
        m = m * jnp.where(idx[2] == 0, 1.0, 0.0)
    if x >= CX + 2:
        m = m * jnp.where(idx[3] == 0, 1.0, 0.0)
    return m


def next_kernel(
    idx, vin, xa, xb, ya, yb, rin, dp1_0, w0, dp1_1, w1, w2,
    z, r, v, out_a, out_b,
    w, got, e1, g1, e2, g2,
):
    assemble(idx, w, vin, xa, xb, ya, yb, got)
    z[...] = w[pl.ds(3, CX)]

    def emit(x, total):
        if 1 <= x <= BX:
            image = dp1_0[x - 1] * w[x] - total
            r[x - 1] = rin[x - 1] - (STEP * box_mask(idx, x - 1)) * image

    stencil(WX, 1, lambda x: w[x], emit)
    v[0] = jnp.zeros((ROWS, CZ), F32)
    v[WX - 1] = jnp.zeros((ROWS, CZ), F32)
    vcycle(v.at[pl.ds(1, BX)], r, dp1_0, w0, dp1_1, w1, w2, e1, g1, e2, g2)
    send_x(idx, v, out_a, out_b)


def dots_kernel(idx, vin, xa, xb, ya, yb, dp1_0, z0, z1, r0, r1, r2, z2, u2, sums, w, got):
    assemble(idx, w, vin, xa, xb, ya, yb, got)

    def emit(x, total):
        if 3 <= x < 3 + CX:
            z2[x - 3] = w[x]
            u2[x - 3] = dp1_0[x - 1] * w[x] - total

    stencil(WX, 1, lambda x: w[x], emit)
    row = rows()
    own = jnp.where((row >= 3) & (row < 3 + CY), 1.0, 0.0)
    acc = [jnp.zeros((ROWS, CZ), F32) for _ in range(7)]
    for x in range(CX):
        a0, a1, a2 = z0[x] * own, z1[x] * own, z2[x] * own
        b0, b1, b2 = r0[x + 2], r1[x + 2], r2[x + 2]
        terms = (a0 * b0, a0 * b1, a0 * b2, a1 * b1, a1 * b2, a2 * b2, a2 * u2[x])
        acc = [s + t for s, t in zip(acc, terms)]
    lane = lax.broadcasted_iota(jnp.int32, (1, CZ), 1)
    out = jnp.zeros((1, CZ), F32)
    for k, s in enumerate(acc):
        part = jnp.sum(jnp.sum(s, axis=0, keepdims=True), axis=1, keepdims=True)
        out = out + jnp.where(lane == k, part, 0.0)
    sums[...] = jnp.broadcast_to(out, sums.shape)


def final_kernel(gathered, z0, z1, z2, r0, r1, r2, u2, x_out, r_out):
    row = jnp.sum(gathered[...], axis=0, keepdims=True)
    lane = lax.broadcasted_iota(jnp.int32, (1, CZ), 1)
    m00, m01, m02, m11, m12, m22, h22 = (
        jnp.sum(jnp.where(lane == k, row, 0.0), axis=1, keepdims=True) for k in range(7)
    )
    inv = 1.0 / STEP
    h00, h01, h02 = inv * (m00 - m01), inv * (m01 - m02), inv * (m02 - m12)
    h11, h12 = inv * (m11 - m12), inv * (m12 - m22)
    l10, l20 = h01 / h00, h02 / h00
    d1 = h11 - l10 * h01
    q = h12 - l10 * h02
    l21 = q / d1
    d2 = h22 - l20 * h02 - l21 * q
    y1 = m01 - l10 * m00
    y2 = m02 - l20 * m00 - l21 * y1
    c2 = y2 / d2
    c1 = y1 / d1 - l21 * c2
    c0 = m00 / h00 - l10 * c1 - l20 * c2
    f0, f1 = inv * c0, inv * c1
    for x in range(CX):
        xs = c0 * z0[x] + c1 * z1[x] + c2 * z2[x]
        b0, b1 = r0[x + 2], r1[x + 2]
        rs = b0 - f0 * (b0 - b1) - f1 * (b1 - r2[x + 2]) - c2 * u2[x]
        x_out[x] = xs[3 : 3 + CY, :]
        r_out[x] = rs[3 : 3 + CY, :]


def vmem(n):
    return [pl.BlockSpec(memory_space=pltpu.VMEM) for _ in range(n)]


def call(body, name, n_in, outs, scratch=(), smem=True):
    in_specs = ([pl.BlockSpec(memory_space=pltpu.SMEM)] if smem else []) + vmem(n_in)
    return pl.pallas_call(
        body,
        out_shape=outs,
        in_specs=in_specs,
        out_specs=vmem(len(outs)),
        scratch_shapes=[pltpu.VMEM(s, F32) for s in scratch],
        name=name,
        interpret=INTERPRET,
    )


INTERPRET = False


def pairs(n_gx, n_gy, axis, odd):
    count = n_gx if axis == 0 else n_gy
    result = []
    for i in range(n_gx):
        for j in range(n_gy):
            here = i if axis == 0 else j
            there = ((here + odd) ^ 1) - odd
            if 0 <= there < count:
                target = (there, j) if axis == 0 else (i, there)
                result.append((i * n_gy + j, target[0] * n_gy + target[1]))
    return result


def solution(mesh):
    n_gx, n_gy = mesh.shape["gx"], mesh.shape["gy"]

    def swap(a, b, axis):
        return (
            lax.ppermute(a, AX, pairs(n_gx, n_gy, axis, 0)),
            lax.ppermute(b, AX, pairs(n_gx, n_gy, axis, 1)),
        )

    box = sds(BX, ROWS, CZ)
    half = sds(BX // 2, ROWS, CZ)
    quarter = sds(BX // 4, ROWS, CZ)
    wide = sds(WX, ROWS, CZ)
    band = sds(YBAND, ROWS, CZ)
    yband = sds(YROWS, CZ)
    own = sds(CX, ROWS, CZ)
    coarse = [half.shape, half.shape, quarter.shape, quarter.shape]

    def on_device(right_side, shift):
        gx, gy = lax.axis_index("gx"), lax.axis_index("gy")
        idx = jnp.stack(
            [gx % 2, gy % 2]
            + [(c).astype(jnp.int32) for c in (gx == 0, gx == n_gx - 1, gy == 0, gy == n_gy - 1)]
        )

        def exchange_y(v, xa, xb):
            return swap(
                *call(
                    pack_y_kernel, "pack_y", 3, [yband, yband], [(WX, 16, CZ), (2, YROWS, CZ)]
                )(idx, v, xa, xb),
                1,
            )

        first = sds(2, 2, CY, CZ)
        xa, xb = swap(*call(pack_x_kernel, "pack_x", 2, [first, first])(idx, right_side, shift), 0)
        strip = sds(IROWS, CZ)
        rbox, sbox, ya, yb = call(
            box_kernel, "box", 4, [box, box, strip, strip], [(2, IROWS, CZ)]
        )(idx, right_side, shift, xa, xb)
        ya, yb = swap(ya, yb, 1)
        r0, v, xa, xb, *coefs = call(
            first_kernel,
            "first",
            4,
            [box, wide, band, band, box, box, half, half, quarter],
            [(2, IROWS, CZ), box.shape, half.shape] + coarse,
        )(idx, rbox, sbox, ya, yb)
        residuals, images = [r0], []
        for step in range(2):
            xa, xb = swap(xa, xb, 0)
            ya, yb = exchange_y(v, xa, xb)
            z, r, v, xa, xb = call(
                next_kernel,
                "next",
                11,
                [own, box, wide, band, band],
                [wide.shape, (2, YROWS, CZ)] + coarse,
            )(idx, v, xa, xb, ya, yb, residuals[-1], *coefs)
            images.append(z)
            residuals.append(r)
        xa, xb = swap(xa, xb, 0)
        ya, yb = exchange_y(v, xa, xb)
        z2, u2, sums = call(
            dots_kernel,
            "dots",
            11,
            [own, own, sds(n_gx * n_gy, CZ)],
            [wide.shape, (2, YROWS, CZ)],
        )(idx, v, xa, xb, ya, yb, coefs[0], *images, *residuals)
        gathered = lax.all_to_all(sums, AX, 0, 0, tiled=True)
        x, r = call(
            final_kernel, "final", 8, [sds(CX, CY, CZ), sds(CX, CY, CZ)], smem=False
        )(gathered, *images, z2, *residuals, u2)
        return x, r

    spec = P("gx", "gy", None)
    return jax.shard_map(
        on_device, mesh=mesh, in_specs=(spec, spec), out_specs=(spec, spec), check_vma=False
    )
```

time: 490 us -> 132 us (0.27)
  the two profiles are of different devices: /device:TPU:42 before, /device:TPU:1 now
where the time goes in v1:
time: 132 us
  starting transfers between devices  45.7 us (35%)
  Pallas kernels  32.9 us (25%)
  blocking collectives  32.3 us (24%)
  waiting for transfers between devices  14.2 us (11%)
  local copies, waits for them, and re-layouts  5.86 us (4%)
    all_to_all x1, blocking collectives, on_device(): gathered = lax.all_to_all(sums, AX, 0, 0, tiled=True)  32.3 us
    ppermute x8, starting transfers between devices, swap(): lax.ppermute(a, AX, pairs(n_gx, n_gy, axis, 0))  24.7 us
    ppermute x8, starting transfers between devices, swap(): lax.ppermute(b, AX, pairs(n_gx, n_gy, axis, 1))  21 us
    pallas_call x2, Pallas kernels, on_device(): call(next_kernel, 'next', 11, [own, box, wide, band, band], [wide.shape,...  12.3 us
    ppermute x8, waiting for transfers between devices, swap(): lax.ppermute(b, AX, pairs(n_gx, n_gy, axis, 1))  9.79 us
    pallas_call x1, Pallas kernels, on_device(): call(first_kernel, 'first', 4, [box, wide, band, band, box, box, half, ha...  5.54 us
    pallas_call x3, Pallas kernels, exchange_y(): call(pack_y_kernel, 'pack_y', 3, [yband, yband], [(WX, 16, CZ), (2, YROWS...  5.42 us
    unnamed x32, local copies, waits for them, and re-layouts  5.2 us
  transfers between devices with their start and end apart: 16, of which 8 were waited for; matrix products, arithmetic and copies ran while one was open for 0% of the time, Pallas kernels for 0%

profile of v1, /device:TPU:1, one launch (start us, length us, event | category | flops | bytes accessed | tf_op | source)
XLA Modules:
  0.0 131.8 jit_solution(11346821028677723747)
XLA Ops:
  1.3 1.7 %pack_x.1 = (f32[2,2,32,128]{3,2,1,0:T(8,128)}, f32[2,2,32,128]{3,2,1,0:T(8,128)}) custom-call(s32[6]{0:T(128)} %stack.43.idx, f32[16,32,128]{2,1,0:T(8,128)} %r.3, f32[16,32,128]{2,1,0:T(8,128)} %s.3), custom_call_target="tpu_custom_call" | custom-call | tf_op jit(solution)/shard_map/pack_x/pallas_call | solution.py:378
  3.0 1.4 %collective-permute-start = (f32[2,2,32,128]{3,2,1,0:T(8,128)}, f32[2,2,32,128]{3,2,1,0:T(8,128)S(1)}, u32[]{:S(2)}, u32[]{:S(2)}) collective-permute-start(f32[2,2,32,128]{3,2,1,0:T(8,128)} %get-tuple-element.36), channel_id=1, source_target_pairs={{0,8},{1,9},{2,10},{3,11},{4,12},{5,13},{6,14},{7,15},{8,0},{9,1},... | collective-permute-start | bytes 196616 | tf_op jit(solution)/shard_map/ppermute | solution.py:349
  4.4 3.5 %collective-permute-start.1 = (f32[2,2,32,128]{3,2,1,0:T(8,128)}, f32[2,2,32,128]{3,2,1,0:T(8,128)S(1)}, u32[]{:S(2)}, u32[]{:S(2)}) collective-permute-start(f32[2,2,32,128]{3,2,1,0:T(8,128)} %get-tuple-element.37), channel_id=1, source_target_pairs={{8,16},{9,17},{10,18},{11,19},{12,20},{13,21},{14,22},{15,23},{16,... | collective-permute-start | bytes 196616 | tf_op jit(solution)/shard_map/ppermute | solution.py:350
  8.0 2.2 %collective-permute-done.1.in_b = f32[2,2,32,128]{3,2,1,0:T(8,128)S(1)} collective-permute-done((f32[2,2,32,128]{3,2,1,0:T(8,128)}, f32[2,2,32,128]{3,2,1,0:T(8,128)S(1)}, u32[]{:S(2)}, u32[]{:S(2)}) %collective-permute-start.1) | collective-permute-done | bytes 65568 | tf_op jit(solution)/shard_map/ppermute | solution.py:350
  10.8 2.0 %box.1 = (f32[20,40,128]{2,1,0:T(8,128)}, f32[20,40,128]{2,1,0:T(8,128)}, f32[80,128]{1,0:T(8,128)}, f32[80,128]{1,0:T(8,128)}) custom-call(s32[6]{0:T(128)} %stack.43.idx, f32[16,32,128]{2,1,0:T(8,128)} %r.3, f32[16,32,128]{2,1,0:T(8,128)} %s.3, f32[2,2,32,128]{3,2,1,0:T(8,128)} %copy-done.6, f32[2,2,32,128]{3,2,1,0:T(8,128)} %copy-done.7), custom_call_target="tpu_custom_call" | custom-call | tf_op jit(solution)/shard_map/box/pallas_call | solution.py:380
  12.8 2.9 %collective-permute-start.2 = (f32[80,128]{1,0:T(8,128)}, f32[80,128]{1,0:T(8,128)S(1)}, u32[]{:S(2)}, u32[]{:S(2)}) collective-permute-start(f32[80,128]{1,0:T(8,128)} %get-tuple-element.40), channel_id=1, source_target_pairs={{0,1},{1,0},{2,3},{3,2},{4,5},{5,4},{6,7},{7,6},{8,9},{9,8},{10,11... | collective-permute-start | bytes 122888 | tf_op jit(solution)/shard_map/ppermute | solution.py:349
  18.1 5.5 %first.1 = (f32[20,40,128]{2,1,0:T(8,128)}, f32[22,40,128]{2,1,0:T(8,128)}, f32[5,40,128]{2,1,0:T(8,128)}, f32[5,40,128]{2,1,0:T(8,128)}, f32[20,40,128]{2,1,0:T...) custom-call(s32[6]{0:T(128)} %stack.43.idx, ...), custom_call_target="tpu_custom_call" | custom-call | tf_op jit(solution)/shard_map/first/pallas_call | solution.py:384
  23.6 4.7 %collective-permute-start.5 = (f32[5,40,128]{2,1,0:T(8,128)}, f32[5,40,128]{2,1,0:T(8,128)S(1)}, u32[]{:S(2)}, u32[]{:S(2)}) collective-permute-start(f32[5,40,128]{2,1,0:T(8,128)} %get-tuple-element.44), channel_id=1, source_target_pairs={{8,16},{9,17},{10,18},{11,19},{12,20},{13,21},{14,22},{15,23},{16,... | collective-permute-start | bytes 307208 | tf_op jit(solution)/shard_map/ppermute | solution.py:350
  28.4 2.5 %collective-permute-done.5.in_b.xb = f32[5,40,128]{2,1,0:T(8,128)S(1)} collective-permute-done((f32[5,40,128]{2,1,0:T(8,128)}, f32[5,40,128]{2,1,0:T(8,128)S(1)}, u32[]{:S(2)}, u32[]{:S(2)}) %collective-permute-start.5) | collective-permute-done | bytes 102432 | tf_op jit(solution)/shard_map/ppermute | solution.py:350
  31.5 1.8 %pack_y.3 = (f32[112,128]{1,0:T(8,128)}, f32[112,128]{1,0:T(8,128)}) custom-call(s32[6]{0:T(128)} %stack.43.idx, f32[22,40,128]{2,1,0:T(8,128)} %get-tuple-element.42.v.vin, f32[5,40,128]{2,1,0:T(8,128)} %copy-done.2, f32[5,40,128]{2,1,0:T(8,128)} %copy-done.5), custom_call_target="tpu_custom_call" | custom-call | tf_op jit(solution)/shard_map/pack_y/pallas_call | solution.py:371
  33.3 6.0 %collective-permute-start.6 = (f32[112,128]{1,0:T(8,128)}, f32[112,128]{1,0:T(8,128)S(1)}, u32[]{:S(2)}, u32[]{:S(2)}) collective-permute-start(f32[112,128]{1,0:T(8,128)} %get-tuple-element.45), channel_id=1, source_target_pairs={{0,1},{1,0},{2,3},{3,2},{4,5},{5,4},{6,7},{7,6},{8,9},{9,8},{10,11... | collective-permute-start | bytes 172040 | tf_op jit(solution)/shard_map/ppermute | solution.py:349
  41.8 6.1 %next.2 = (f32[16,40,128]{2,1,0:T(8,128)}, f32[20,40,128]{2,1,0:T(8,128)}, f32[22,40,128]{2,1,0:T(8,128)}, f32[5,40,128]{2,1,0:T(8,128)}, f32[5,40,128]{2,1,0:T(8,128)}) custom-call(s32[6]{0:T(128)} %stack.43.idx, f32[22,40,128]{2,1,0:T(8,128)} %get-tuple-element.42.v.vin, f32[5,40,128]{2,1,0:T(8,128)} %copy-done.2, f32[5,40,128]{2,1,0:T(8,128)} %copy-done.5, ...), custom_call_target="tpu_custom_call" | custom-call | tf_op jit(solution)/shard_map/next/pallas_call | solution.py:395
  47.9 4.9 %collective-permute-start.9 = (f32[5,40,128]{2,1,0:T(8,128)}, f32[5,40,128]{2,1,0:T(8,128)S(1)}, u32[]{:S(2)}, u32[]{:S(2)}) collective-permute-start(f32[5,40,128]{2,1,0:T(8,128)} %get-tuple-element.55), channel_id=1, source_target_pairs={{8,16},{9,17},{10,18},{11,19},{12,20},{13,21},{14,22},{15,23},{16,... | collective-permute-start | bytes 307208 | tf_op jit(solution)/shard_map/ppermute | solution.py:350
  52.9 2.5 %collective-permute-done.9.in_b.xb = f32[5,40,128]{2,1,0:T(8,128)S(1)} collective-permute-done((f32[5,40,128]{2,1,0:T(8,128)}, f32[5,40,128]{2,1,0:T(8,128)S(1)}, u32[]{:S(2)}, u32[]{:S(2)}) %collective-permute-start.9) | collective-permute-done | bytes 102432 | tf_op jit(solution)/shard_map/ppermute | solution.py:350
  56.0 1.8 %pack_y.4 = (f32[112,128]{1,0:T(8,128)}, f32[112,128]{1,0:T(8,128)}) custom-call(s32[6]{0:T(128)} %stack.43.idx, f32[22,40,128]{2,1,0:T(8,128)} %get-tuple-element.53.v.vin, f32[5,40,128]{2,1,0:T(8,128)} %copy-done, f32[5,40,128]{2,1,0:T(8,128)} %copy-done.3), custom_call_target="tpu_custom_call" | custom-call | tf_op jit(solution)/shard_map/pack_y/pallas_call | solution.py:371
  57.8 5.8 %collective-permute-start.10 = (f32[112,128]{1,0:T(8,128)}, f32[112,128]{1,0:T(8,128)S(1)}, u32[]{:S(2)}, u32[]{:S(2)}) collective-permute-start(f32[112,128]{1,0:T(8,128)} %get-tuple-element.56), channel_id=1, source_target_pairs={{0,1},{1,0},{2,3},{3,2},{4,5},{5,4},{6,7},{7,6},{8,9},{9,8},{10,11... | collective-permute-start | bytes 172040 | tf_op jit(solution)/shard_map/ppermute | solution.py:349
  66.1 6.2 %next.3 = (f32[16,40,128]{2,1,0:T(8,128)}, f32[20,40,128]{2,1,0:T(8,128)}, f32[22,40,128]{2,1,0:T(8,128)}, f32[5,40,128]{2,1,0:T(8,128)}, f32[5,40,128]{2,1,0:T(8,128)}) custom-call(s32[6]{0:T(128)} %stack.43.idx, f32[22,40,128]{2,1,0:T(8,128)} %get-tuple-element.53.v.vin, f32[5,40,128]{2,1,0:T(8,128)} %copy-done, f32[5,40,128]{2,1,0:T(8,128)} %copy-done.3, ...), custom_call_target="tpu_custom_call" | custom-call | tf_op jit(solution)/shard_map/next/pallas_call | solution.py:395
  72.3 5.2 %collective-permute-start.13 = (f32[5,40,128]{2,1,0:T(8,128)}, f32[5,40,128]{2,1,0:T(8,128)S(1)}, u32[]{:S(2)}, u32[]{:S(2)}) collective-permute-start(f32[5,40,128]{2,1,0:T(8,128)} %get-tuple-element.61), channel_id=1, source_target_pairs={{8,16},{9,17},{10,18},{11,19},{12,20},{13,21},{14,22},{15,23},{16,... | collective-permute-start | bytes 307208 | tf_op jit(solution)/shard_map/ppermute | solution.py:350
  77.6 2.5 %collective-permute-done.13.in_b.xb = f32[5,40,128]{2,1,0:T(8,128)S(1)} collective-permute-done((f32[5,40,128]{2,1,0:T(8,128)}, f32[5,40,128]{2,1,0:T(8,128)S(1)}, u32[]{:S(2)}, u32[]{:S(2)}) %collective-permute-start.13) | collective-permute-done | bytes 102432 | tf_op jit(solution)/shard_map/ppermute | solution.py:350
  80.7 1.8 %pack_y.5 = (f32[112,128]{1,0:T(8,128)}, f32[112,128]{1,0:T(8,128)}) custom-call(s32[6]{0:T(128)} %stack.43.idx, f32[22,40,128]{2,1,0:T(8,128)} %get-tuple-element.59.v.vin, f32[5,40,128]{2,1,0:T(8,128)} %copy-done.1, f32[5,40,128]{2,1,0:T(8,128)} %copy-done.4), custom_call_target="tpu_custom_call" | custom-call | tf_op jit(solution)/shard_map/pack_y/pallas_call | solution.py:371
  82.5 8.7 %collective-permute-start.14 = (f32[112,128]{1,0:T(8,128)}, f32[112,128]{1,0:T(8,128)S(1)}, u32[]{:S(2)}, u32[]{:S(2)}) collective-permute-start(f32[112,128]{1,0:T(8,128)} %get-tuple-element.62), channel_id=1, source_target_pairs={{0,1},{1,0},{2,3},{3,2},{4,5},{5,4},{6,7},{7,6},{8,9},{9,8},{10,11... | collective-permute-start | bytes 172040 | tf_op jit(solution)/shard_map/ppermute | solution.py:349
  93.7 3.2 %dots.1 = (f32[16,40,128]{2,1,0:T(8,128)}, f32[16,40,128]{2,1,0:T(8,128)}, f32[128,128]{1,0:T(8,128)}) custom-call(s32[6]{0:T(128)} %stack.43.idx, f32[22,40,128]{2,1,0:T(8,128)} %get-tuple-element.59.v.vin, f32[5,40,128]{2,1,0:T(8,128)} %copy-done.1, f32[5,40,128]{2,1,0:T(8,128)} %copy-done.4, f32[112,128]{1,0:T(8,128)} %copy-done.9, ...), custom_call_target="tpu_custom_call" | custom-call | tf_op jit(solution)/shard_map/dots/pallas_call | solution.py:406
  96.8 32.3 %all_to_all.11 = f32[128,1,128]{2,1,0:T(1,128)} all-to-all(f32[128,1,128]{2,1,0:T(1,128)} %bitcast.11), channel_id=1, replica_groups=mesh['gx'=16,'gy'=8] {'gx','gy'}, dimensions={0} | all-to-all | bytes 131072 | tf_op jit(solution)/shard_map/all_to_all | solution.py:413
  129.1 2.7 %final.1 = (f32[16,32,128]{2,1,0:T(8,128)}, f32[16,32,128]{2,1,0:T(8,128)}) custom-call(f32[128,128]{1,0:T(8,128)} %bitcast.10, f32[16,40,128]{2,1,0:T(8,128)} %get-tuple-element.64.z0, f32[16,40,128]{2,1,0:T(8,128)} %get-tuple-element.65.z1, f32[16,40,128]{2,1,0:T(8,128)} %get-tuple-element.68.z2, f32[20,40,128]{2,1,0:T(8,128)} %get-tuple-element.47.rin.r0, ...), custom_call_target="tpu_custom_call" | custom-call | tf_op jit(solution)/shard_map/final/pallas_call | solution.py:414
  (52 shorter events, 12.9 us)
Async XLA Ops:
  3.0 4.9 %collective-permute-start = (f32[2,2,32,128]{3,2,1,0:T(8,128)}, f32[2,2,32,128]{3,2,1,0:T(8,128)S(1)}, u32[]{:S(2)}, u32[]{:S(2)}) collective-permute-start(f32[2,2,32,128]{3,2,1,0:T(8,128)} %get-tuple-element.36), channel_id=1, source_target_pairs={{0,8},{1,9},{2,10},{3,11},{4,12},{5,13},{6,14},{7,15},{8,0},{9,1},... | collective-permute-start | bytes 196616 | tf_op jit(solution)/shard_map/ppermute | solution.py:349
  4.4 5.8 %collective-permute-start.1 = (f32[2,2,32,128]{3,2,1,0:T(8,128)}, f32[2,2,32,128]{3,2,1,0:T(8,128)S(1)}, u32[]{:S(2)}, u32[]{:S(2)}) collective-permute-start(f32[2,2,32,128]{3,2,1,0:T(8,128)} %get-tuple-element.37), channel_id=1, source_target_pairs={{8,16},{9,17},{10,18},{11,19},{12,20},{13,21},{14,22},{15,23},{16,... | collective-permute-start | bytes 196616 | tf_op jit(solution)/shard_map/ppermute | solution.py:350
  8.0 2.2 %copy-start.6 = (f32[2,2,32,128]{3,2,1,0:T(8,128)}, f32[2,2,32,128]{3,2,1,0:T(8,128)S(1)}, u32[]{:S(2)}) copy-start(f32[2,2,32,128]{3,2,1,0:T(8,128)S(1)} %collective-permute-done.in_a) | copy-start | bytes 196612
  12.8 4.6 %collective-permute-start.2 = (f32[80,128]{1,0:T(8,128)}, f32[80,128]{1,0:T(8,128)S(1)}, u32[]{:S(2)}, u32[]{:S(2)}) collective-permute-start(f32[80,128]{1,0:T(8,128)} %get-tuple-element.40), channel_id=1, source_target_pairs={{0,1},{1,0},{2,3},{3,2},{4,5},{5,4},{6,7},{7,6},{8,9},{9,8},{10,11... | collective-permute-start | bytes 122888 | tf_op jit(solution)/shard_map/ppermute | solution.py:349
  15.7 1.7 %collective-permute-start.3 = (f32[80,128]{1,0:T(8,128)}, f32[80,128]{1,0:T(8,128)S(1)}, u32[]{:S(2)}, u32[]{:S(2)}) collective-permute-start(f32[80,128]{1,0:T(8,128)} %get-tuple-element.41), channel_id=1, source_target_pairs={{1,2},{2,1},{3,4},{4,3},{5,6},{6,5},{9,10},{10,9},{11,12},{12,11},... | collective-permute-start | bytes 122888 | tf_op jit(solution)/shard_map/ppermute | solution.py:350
  17.4 0.7 copy-start.15
  23.6 4.7 %collective-permute-start.4 = (f32[5,40,128]{2,1,0:T(8,128)}, f32[5,40,128]{2,1,0:T(8,128)S(1)}, u32[]{:S(2)}, u32[]{:S(2)}) collective-permute-start(f32[5,40,128]{2,1,0:T(8,128)} %get-tuple-element.43), channel_id=1, source_target_pairs={{0,8},{1,9},{2,10},{3,11},{4,12},{5,13},{6,14},{7,15},{8,0},{9,1},... | collective-permute-start | bytes 307208 | tf_op jit(solution)/shard_map/ppermute | solution.py:349
  23.6 7.2 %collective-permute-start.5 = (f32[5,40,128]{2,1,0:T(8,128)}, f32[5,40,128]{2,1,0:T(8,128)S(1)}, u32[]{:S(2)}, u32[]{:S(2)}) collective-permute-start(f32[5,40,128]{2,1,0:T(8,128)} %get-tuple-element.44), channel_id=1, source_target_pairs={{8,16},{9,17},{10,18},{11,19},{12,20},{13,21},{14,22},{15,23},{16,... | collective-permute-start | bytes 307208 | tf_op jit(solution)/shard_map/ppermute | solution.py:350
  28.3 2.5 %copy-start.2 = (f32[5,40,128]{2,1,0:T(8,128)}, f32[5,40,128]{2,1,0:T(8,128)S(1)}, u32[]{:S(2)}) copy-start(f32[5,40,128]{2,1,0:T(8,128)S(1)} %collective-permute-done.4.in_a.xa) | copy-start | bytes 307204
  33.3 7.8 %collective-permute-start.6 = (f32[112,128]{1,0:T(8,128)}, f32[112,128]{1,0:T(8,128)S(1)}, u32[]{:S(2)}, u32[]{:S(2)}) collective-permute-start(f32[112,128]{1,0:T(8,128)} %get-tuple-element.45), channel_id=1, source_target_pairs={{0,1},{1,0},{2,3},{3,2},{4,5},{5,4},{6,7},{7,6},{8,9},{9,8},{10,11... | collective-permute-start | bytes 172040 | tf_op jit(solution)/shard_map/ppermute | solution.py:349
  39.3 1.8 %collective-permute-start.7 = (f32[112,128]{1,0:T(8,128)}, f32[112,128]{1,0:T(8,128)S(1)}, u32[]{:S(2)}, u32[]{:S(2)}) collective-permute-start(f32[112,128]{1,0:T(8,128)} %get-tuple-element.46), channel_id=1, source_target_pairs={{1,2},{2,1},{3,4},{4,3},{5,6},{6,5},{9,10},{10,9},{11,12},{12,11},... | collective-permute-start | bytes 172040 | tf_op jit(solution)/shard_map/ppermute | solution.py:350
  47.9 4.9 %collective-permute-start.8 = (f32[5,40,128]{2,1,0:T(8,128)}, f32[5,40,128]{2,1,0:T(8,128)S(1)}, u32[]{:S(2)}, u32[]{:S(2)}) collective-permute-start(f32[5,40,128]{2,1,0:T(8,128)} %get-tuple-element.54), channel_id=1, source_target_pairs={{0,8},{1,9},{2,10},{3,11},{4,12},{5,13},{6,14},{7,15},{8,0},{9,1},... | collective-permute-start | bytes 307208 | tf_op jit(solution)/shard_map/ppermute | solution.py:349
  47.9 7.5 %collective-permute-start.9 = (f32[5,40,128]{2,1,0:T(8,128)}, f32[5,40,128]{2,1,0:T(8,128)S(1)}, u32[]{:S(2)}, u32[]{:S(2)}) collective-permute-start(f32[5,40,128]{2,1,0:T(8,128)} %get-tuple-element.55), channel_id=1, source_target_pairs={{8,16},{9,17},{10,18},{11,19},{12,20},{13,21},{14,22},{15,23},{16,... | collective-permute-start | bytes 307208 | tf_op jit(solution)/shard_map/ppermute | solution.py:350
  52.8 2.5 %copy-start = (f32[5,40,128]{2,1,0:T(8,128)}, f32[5,40,128]{2,1,0:T(8,128)S(1)}, u32[]{:S(2)}) copy-start(f32[5,40,128]{2,1,0:T(8,128)S(1)} %collective-permute-done.8.in_a.xa) | copy-start | bytes 307204
  55.4 0.7 copy-start.3
  57.8 7.6 %collective-permute-start.10 = (f32[112,128]{1,0:T(8,128)}, f32[112,128]{1,0:T(8,128)S(1)}, u32[]{:S(2)}, u32[]{:S(2)}) collective-permute-start(f32[112,128]{1,0:T(8,128)} %get-tuple-element.56), channel_id=1, source_target_pairs={{0,1},{1,0},{2,3},{3,2},{4,5},{5,4},{6,7},{7,6},{8,9},{9,8},{10,11... | collective-permute-start | bytes 172040 | tf_op jit(solution)/shard_map/ppermute | solution.py:349
  63.7 1.8 %collective-permute-start.11 = (f32[112,128]{1,0:T(8,128)}, f32[112,128]{1,0:T(8,128)S(1)}, u32[]{:S(2)}, u32[]{:S(2)}) collective-permute-start(f32[112,128]{1,0:T(8,128)} %get-tuple-element.57), channel_id=1, source_target_pairs={{1,2},{2,1},{3,4},{4,3},{5,6},{6,5},{9,10},{10,9},{11,12},{12,11},... | collective-permute-start | bytes 172040 | tf_op jit(solution)/shard_map/ppermute | solution.py:350
  65.5 0.7 copy-start.11
  72.3 5.2 %collective-permute-start.12 = (f32[5,40,128]{2,1,0:T(8,128)}, f32[5,40,128]{2,1,0:T(8,128)S(1)}, u32[]{:S(2)}, u32[]{:S(2)}) collective-permute-start(f32[5,40,128]{2,1,0:T(8,128)} %get-tuple-element.60), channel_id=1, source_target_pairs={{0,8},{1,9},{2,10},{3,11},{4,12},{5,13},{6,14},{7,15},{8,0},{9,1},... | collective-permute-start | bytes 307208 | tf_op jit(solution)/shard_map/ppermute | solution.py:349
  72.3 7.8 %collective-permute-start.13 = (f32[5,40,128]{2,1,0:T(8,128)}, f32[5,40,128]{2,1,0:T(8,128)S(1)}, u32[]{:S(2)}, u32[]{:S(2)}) collective-permute-start(f32[5,40,128]{2,1,0:T(8,128)} %get-tuple-element.61), channel_id=1, source_target_pairs={{8,16},{9,17},{10,18},{11,19},{12,20},{13,21},{14,22},{15,23},{16,... | collective-permute-start | bytes 307208 | tf_op jit(solution)/shard_map/ppermute | solution.py:350
  77.6 2.5 %copy-start.1 = (f32[5,40,128]{2,1,0:T(8,128)}, f32[5,40,128]{2,1,0:T(8,128)S(1)}, u32[]{:S(2)}) copy-start(f32[5,40,128]{2,1,0:T(8,128)S(1)} %collective-permute-done.12.in_a.xa) | copy-start | bytes 307204
  82.5 10.5 %collective-permute-start.14 = (f32[112,128]{1,0:T(8,128)}, f32[112,128]{1,0:T(8,128)S(1)}, u32[]{:S(2)}, u32[]{:S(2)}) collective-permute-start(f32[112,128]{1,0:T(8,128)} %get-tuple-element.62), channel_id=1, source_target_pairs={{0,1},{1,0},{2,3},{3,2},{4,5},{5,4},{6,7},{7,6},{8,9},{9,8},{10,11... | collective-permute-start | bytes 172040 | tf_op jit(solution)/shard_map/ppermute | solution.py:349
  91.2 1.8 %collective-permute-start.15 = (f32[112,128]{1,0:T(8,128)}, f32[112,128]{1,0:T(8,128)S(1)}, u32[]{:S(2)}, u32[]{:S(2)}) collective-permute-start(f32[112,128]{1,0:T(8,128)} %get-tuple-element.63), channel_id=1, source_target_pairs={{1,2},{2,1},{3,4},{4,3},{5,6},{6,5},{9,10},{10,9},{11,12},{12,11},... | collective-permute-start | bytes 172040 | tf_op jit(solution)/shard_map/ppermute | solution.py:350
  93.0 0.7 copy-start.12
  (8 other events, 5.1 us)

commit v2 on v1

--- a/solution.py
+++ b/solution.py
@@ -322,10 +322,12 @@
         scratch_shapes=[pltpu.VMEM(s, F32) for s in scratch],
         name=name,
         interpret=INTERPRET,
+        compiler_params=pltpu.CompilerParams(vmem_limit_bytes=VMEM_LIMIT),
     )
 
 
 INTERPRET = False
+VMEM_LIMIT = 16 * 2**20
 
 
 def pairs(n_gx, n_gy, axis, odd):

time: 132 us -> 112 us (0.85)
  Pallas kernels: 32.9 us -> 17.6 us
  local copies, waits for them, and re-layouts: 5.86 us -> 1.99 us
  waiting for transfers between devices: 14.2 us -> 12.5 us
    pallas_call x2, Pallas kernels: 12.3 us -> 8.23 us  [on_device(): call(next_kernel, 'next', 11, [own, box, wide, band, band], [wide.shape,...]
    pallas_call x3, Pallas kernels: 5.42 us -> 1.78 us  [exchange_y(): call(pack_y_kernel, 'pack_y', 3, [yband, yband], [(WX, 16, CZ), (2, YROWS...]
    unnamed x32 -> x4, local copies, waits for them, and re-layouts: 5.2 us -> 1.9 us
    pallas_call x1, Pallas kernels: 3.18 us -> 1.3 us  [on_device(): call(dots_kernel, 'dots', 11, [own, own, sds(n_gx * n_gy, CZ)], [wide.sha...]
    pallas_call x1, Pallas kernels: 2.72 us -> 1.1 us  [on_device(): call(final_kernel, 'final', 8, [sds(CX, CY, CZ), sds(CX, CY, CZ)], smem=F...]
    pallas_call x1, Pallas kernels: 5.54 us -> 3.99 us  [on_device(): call(first_kernel, 'first', 4, [box, wide, band, band, box, box, half, ha...]
    pallas_call x1, Pallas kernels: 2.03 us -> 0.67 us  [on_device(): call(box_kernel, 'box', 4, [box, box, strip, strip], [(2, IROWS, CZ)])]
where the time goes in v2:
time: 112 us; the launch traced here: 111 us
  starting transfers between devices  46.5 us (42%)
  blocking collectives  31.8 us (28%)
  Pallas kernels  17.6 us (16%)
  waiting for transfers between devices  12.5 us (11%)
  local copies, waits for them, and re-layouts  1.99 us (2%)
    all_to_all x1, blocking collectives, on_device(): gathered = lax.all_to_all(sums, AX, 0, 0, tiled=True)  31.8 us
    ppermute x8, starting transfers between devices, swap(): lax.ppermute(a, AX, pairs(n_gx, n_gy, axis, 0))  25.9 us
    ppermute x8, starting transfers between devices, swap(): lax.ppermute(b, AX, pairs(n_gx, n_gy, axis, 1))  20.6 us
    ppermute x8, waiting for transfers between devices, swap(): lax.ppermute(b, AX, pairs(n_gx, n_gy, axis, 1))  8.97 us
    pallas_call x2, Pallas kernels, on_device(): call(next_kernel, 'next', 11, [own, box, wide, band, band], [wide.shape,...  8.23 us
    pallas_call x1, Pallas kernels, on_device(): call(first_kernel, 'first', 4, [box, wide, band, band, box, box, half, ha...  3.99 us
    ppermute x8, waiting for transfers between devices, swap(): lax.ppermute(a, AX, pairs(n_gx, n_gy, axis, 0))  3.58 us
  transfers between devices with their start and end apart: 16, of which 8 were waited for; matrix products, arithmetic and copies ran while one was open for 0% of the time, Pallas kernels for 0%

profile of v2, /device:TPU:1, one launch (start us, length us, event | category | flops | bytes accessed | tf_op | source)
XLA Modules:
  0.0 111.3 jit_solution(10885100799961698334)
XLA Ops:
  0.7 1.0 copy-done
  1.7 0.9 copy-done.1
  3.2 1.5 %collective-permute-start = (f32[2,2,32,128]{3,2,1,0:T(8,128)S(1)}, f32[2,2,32,128]{3,2,1,0:T(8,128)S(1)}, u32[]{:S(2)}, u32[]{:S(2)}) collective-permute-start(f32[2,2,32,128]{3,2,1,0:T(8,128)S(1)} %get-tuple-element.36), channel_id=1, source_target_pairs={{0,8},{1,9},{2,10},{3,11},{4,12},{5,13},{6,14},{7,15},{8,0},{9,1},... | collective-permute-start | bytes 196616 | tf_op jit(solution)/shard_map/ppermute | solution.py:351
  4.7 3.6 %collective-permute-start.1 = (f32[2,2,32,128]{3,2,1,0:T(8,128)S(1)}, f32[2,2,32,128]{3,2,1,0:T(8,128)S(1)}, u32[]{:S(2)}, u32[]{:S(2)}) collective-permute-start(f32[2,2,32,128]{3,2,1,0:T(8,128)S(1)} %get-tuple-element.37), channel_id=1, source_target_pairs={{8,16},{9,17},{10,18},{11,19},{12,20},{13,21},{14,22},{15,23},{16,... | collective-permute-start | bytes 196616 | tf_op jit(solution)/shard_map/ppermute | solution.py:352
  8.2 2.0 %collective-permute-done.1.in_b = f32[2,2,32,128]{3,2,1,0:T(8,128)S(1)} collective-permute-done((f32[2,2,32,128]{3,2,1,0:T(8,128)S(1)}, f32[2,2,32,128]{3,2,1,0:T(8,128)S(1)}, u32[]{:S(2)}, u32[]{:S(2)}) %collective-permute-start.1) | collective-permute-done | bytes 65568 | tf_op jit(solution)/shard_map/ppermute | solution.py:352
  10.9 2.9 %collective-permute-start.2 = (f32[80,128]{1,0:T(8,128)S(1)}, f32[80,128]{1,0:T(8,128)S(1)}, u32[]{:S(2)}, u32[]{:S(2)}) collective-permute-start(f32[80,128]{1,0:T(8,128)S(1)} %get-tuple-element.40), channel_id=1, source_target_pairs={{0,1},{1,0},{2,3},{3,2},{4,5},{5,4},{6,7},{7,6},{8,9},{9,8},{10,11... | collective-permute-start | bytes 122888 | tf_op jit(solution)/shard_map/ppermute | solution.py:351
  15.4 4.0 %first.1 = (f32[20,40,128]{2,1,0:T(8,128)S(1)}, f32[22,40,128]{2,1,0:T(8,128)S(1)}, f32[5,40,128]{2,1,0:T(8,128)S(1)}, f32[5,40,128]{2,1,0:T(8,128)S(1)}, f32[20...) custom-call(s32[6]{0:T(128)S(1)} %stack.43.idx, ...), custom_call_target="tpu_custom_call" | custom-call | tf_op jit(solution)/shard_map/first/pallas_call | solution.py:386
  19.4 4.7 %collective-permute-start.5 = (f32[5,40,128]{2,1,0:T(8,128)S(1)}, f32[5,40,128]{2,1,0:T(8,128)S(1)}, u32[]{:S(2)}, u32[]{:S(2)}) collective-permute-start(f32[5,40,128]{2,1,0:T(8,128)S(1)} %get-tuple-element.44), channel_id=1, source_target_pairs={{8,16},{9,17},{10,18},{11,19},{12,20},{13,21},{14,22},{15,23},{16,... | collective-permute-start | bytes 307208 | tf_op jit(solution)/shard_map/ppermute | solution.py:352
  24.2 2.3 %collective-permute-done.5.in_b.xb = f32[5,40,128]{2,1,0:T(8,128)S(1)} collective-permute-done((f32[5,40,128]{2,1,0:T(8,128)S(1)}, f32[5,40,128]{2,1,0:T(8,128)S(1)}, u32[]{:S(2)}, u32[]{:S(2)}) %collective-permute-start.5) | collective-permute-done | bytes 102432 | tf_op jit(solution)/shard_map/ppermute | solution.py:352
  27.1 6.2 %collective-permute-start.6 = (f32[112,128]{1,0:T(8,128)S(1)}, f32[112,128]{1,0:T(8,128)S(1)}, u32[]{:S(2)}, u32[]{:S(2)}) collective-permute-start(f32[112,128]{1,0:T(8,128)S(1)} %get-tuple-element.45), channel_id=1, source_target_pairs={{0,1},{1,0},{2,3},{3,2},{4,5},{5,4},{6,7},{7,6},{8,9},{9,8},{10,11... | collective-permute-start | bytes 172040 | tf_op jit(solution)/shard_map/ppermute | solution.py:351
  34.0 0.9 collective-permute-done.6.ya
  34.9 4.1 %next.2 = (f32[16,40,128]{2,1,0:T(8,128)S(1)}, f32[20,40,128]{2,1,0:T(8,128)S(1)}, f32[22,40,128]{2,1,0:T(8,128)S(1)}, f32[5,40,128]{2,1,0:T(8,128)S(1)}, f32[5,40,128]{2,1,0:T(8,128)S(1)}) custom-call(s32[6]{0:T(128)S(1)} %stack.43.idx, f32[22,40,128]{2,1,0:T(8,128)S(1)} %get-tuple-element.42.v.vin, f32[5,40,128]{2,1,0:T(8,128)S(1)} %collective-permute-done.4.in_a.xa, ...), custom_call_target="tpu_custom_call" | custom-call | tf_op jit(solution)/shard_map/next/pallas_call | solution.py:397
  39.1 4.8 %collective-permute-start.9 = (f32[5,40,128]{2,1,0:T(8,128)S(1)}, f32[5,40,128]{2,1,0:T(8,128)S(1)}, u32[]{:S(2)}, u32[]{:S(2)}) collective-permute-start(f32[5,40,128]{2,1,0:T(8,128)S(1)} %get-tuple-element.55), channel_id=1, source_target_pairs={{8,16},{9,17},{10,18},{11,19},{12,20},{13,21},{14,22},{15,23},{16,... | collective-permute-start | bytes 307208 | tf_op jit(solution)/shard_map/ppermute | solution.py:352
  43.9 2.3 %collective-permute-done.9.in_b.xb = f32[5,40,128]{2,1,0:T(8,128)S(1)} collective-permute-done((f32[5,40,128]{2,1,0:T(8,128)S(1)}, f32[5,40,128]{2,1,0:T(8,128)S(1)}, u32[]{:S(2)}, u32[]{:S(2)}) %collective-permute-start.9) | collective-permute-done | bytes 102432 | tf_op jit(solution)/shard_map/ppermute | solution.py:352
  46.9 6.2 %collective-permute-start.10 = (f32[112,128]{1,0:T(8,128)S(1)}, f32[112,128]{1,0:T(8,128)S(1)}, u32[]{:S(2)}, u32[]{:S(2)}) collective-permute-start(f32[112,128]{1,0:T(8,128)S(1)} %get-tuple-element.56), channel_id=1, source_target_pairs={{0,1},{1,0},{2,3},{3,2},{4,5},{5,4},{6,7},{7,6},{8,9},{9,8},{10,11... | collective-permute-start | bytes 172040 | tf_op jit(solution)/shard_map/ppermute | solution.py:351
  53.8 0.9 collective-permute-done.10.ya
  54.7 4.1 %next.3 = (f32[16,40,128]{2,1,0:T(8,128)S(1)}, f32[20,40,128]{2,1,0:T(8,128)S(1)}, f32[22,40,128]{2,1,0:T(8,128)S(1)}, f32[5,40,128]{2,1,0:T(8,128)S(1)}, f32[5,40,128]{2,1,0:T(8,128)S(1)}) custom-call(s32[6]{0:T(128)S(1)} %stack.43.idx, f32[22,40,128]{2,1,0:T(8,128)S(1)} %get-tuple-element.53.v.vin, f32[5,40,128]{2,1,0:T(8,128)S(1)} %collective-permute-done.8.in_a.xa, ...), custom_call_target="tpu_custom_call" | custom-call | tf_op jit(solution)/shard_map/next/pallas_call | solution.py:397
  58.9 4.9 %collective-permute-start.13 = (f32[5,40,128]{2,1,0:T(8,128)S(1)}, f32[5,40,128]{2,1,0:T(8,128)S(1)}, u32[]{:S(2)}, u32[]{:S(2)}) collective-permute-start(f32[5,40,128]{2,1,0:T(8,128)S(1)} %get-tuple-element.61), channel_id=1, source_target_pairs={{8,16},{9,17},{10,18},{11,19},{12,20},{13,21},{14,22},{15,23},{16,... | collective-permute-start | bytes 307208 | tf_op jit(solution)/shard_map/ppermute | solution.py:352
  63.8 2.3 %collective-permute-done.13.in_b.xb = f32[5,40,128]{2,1,0:T(8,128)S(1)} collective-permute-done((f32[5,40,128]{2,1,0:T(8,128)S(1)}, f32[5,40,128]{2,1,0:T(8,128)S(1)}, u32[]{:S(2)}, u32[]{:S(2)}) %collective-permute-start.13) | collective-permute-done | bytes 102432 | tf_op jit(solution)/shard_map/ppermute | solution.py:352
  66.7 8.8 %collective-permute-start.14 = (f32[112,128]{1,0:T(8,128)S(1)}, f32[112,128]{1,0:T(8,128)S(1)}, u32[]{:S(2)}, u32[]{:S(2)}) collective-permute-start(f32[112,128]{1,0:T(8,128)S(1)} %get-tuple-element.62), channel_id=1, source_target_pairs={{0,1},{1,0},{2,3},{3,2},{4,5},{5,4},{6,7},{7,6},{8,9},{9,8},{10,11... | collective-permute-start | bytes 172040 | tf_op jit(solution)/shard_map/ppermute | solution.py:351
  76.2 0.9 collective-permute-done.14.ya
  77.1 1.3 %dots.1 = (f32[16,40,128]{2,1,0:T(8,128)S(1)}, f32[16,40,128]{2,1,0:T(8,128)S(1)}, f32[128,128]{1,0:T(8,128)S(1)}) custom-call(s32[6]{0:T(128)S(1)} %stack.43.idx, f32[22,40,128]{2,1,0:T(8,128)S(1)} %get-tuple-element.59.v.vin, f32[5,40,128]{2,1,0:T(8,128)S(1)} %collective-permute-done.12.in_a.xa, f32[5,40,128]{2,1,0:T(8,128)S(1)} %collective-permute-done.13.in_b.xb, ...), custom_call_target="tpu_custom_call" | custom-call | tf_op jit(solution)/shard_map/dots/pallas_call | solution.py:408
  78.4 31.8 %all_to_all.11 = f32[128,1,128]{2,1,0:T(1,128)S(1)} all-to-all(f32[128,1,128]{2,1,0:T(1,128)S(1)} %bitcast.11), channel_id=1, replica_groups=mesh['gx'=16,'gy'=8] {'gx','gy'}, dimensions={0} | all-to-all | bytes 131072 | tf_op jit(solution)/shard_map/all_to_all | solution.py:415
  110.1 1.1 final.1
  (24 shorter events, 6.8 us)
Async XLA Ops:
  0.7 1.0 copy-start
  1.7 0.9 copy-start.1
  3.2 5.0 %collective-permute-start = (f32[2,2,32,128]{3,2,1,0:T(8,128)S(1)}, f32[2,2,32,128]{3,2,1,0:T(8,128)S(1)}, u32[]{:S(2)}, u32[]{:S(2)}) collective-permute-start(f32[2,2,32,128]{3,2,1,0:T(8,128)S(1)} %get-tuple-element.36), channel_id=1, source_target_pairs={{0,8},{1,9},{2,10},{3,11},{4,12},{5,13},{6,14},{7,15},{8,0},{9,1},... | collective-permute-start | bytes 196616 | tf_op jit(solution)/shard_map/ppermute | solution.py:351
  4.7 5.6 %collective-permute-start.1 = (f32[2,2,32,128]{3,2,1,0:T(8,128)S(1)}, f32[2,2,32,128]{3,2,1,0:T(8,128)S(1)}, u32[]{:S(2)}, u32[]{:S(2)}) collective-permute-start(f32[2,2,32,128]{3,2,1,0:T(8,128)S(1)} %get-tuple-element.37), channel_id=1, source_target_pairs={{8,16},{9,17},{10,18},{11,19},{12,20},{13,21},{14,22},{15,23},{16,... | collective-permute-start | bytes 196616 | tf_op jit(solution)/shard_map/ppermute | solution.py:352
  10.9 4.4 %collective-permute-start.2 = (f32[80,128]{1,0:T(8,128)S(1)}, f32[80,128]{1,0:T(8,128)S(1)}, u32[]{:S(2)}, u32[]{:S(2)}) collective-permute-start(f32[80,128]{1,0:T(8,128)S(1)} %get-tuple-element.40), channel_id=1, source_target_pairs={{0,1},{1,0},{2,3},{3,2},{4,5},{5,4},{6,7},{7,6},{8,9},{9,8},{10,11... | collective-permute-start | bytes 122888 | tf_op jit(solution)/shard_map/ppermute | solution.py:351
  13.9 1.5 %collective-permute-start.3 = (f32[80,128]{1,0:T(8,128)S(1)}, f32[80,128]{1,0:T(8,128)S(1)}, u32[]{:S(2)}, u32[]{:S(2)}) collective-permute-start(f32[80,128]{1,0:T(8,128)S(1)} %get-tuple-element.41), channel_id=1, source_target_pairs={{1,2},{2,1},{3,4},{4,3},{5,6},{6,5},{9,10},{10,9},{11,12},{12,11},... | collective-permute-start | bytes 122888 | tf_op jit(solution)/shard_map/ppermute | solution.py:352
  19.3 4.8 %collective-permute-start.4 = (f32[5,40,128]{2,1,0:T(8,128)S(1)}, f32[5,40,128]{2,1,0:T(8,128)S(1)}, u32[]{:S(2)}, u32[]{:S(2)}) collective-permute-start(f32[5,40,128]{2,1,0:T(8,128)S(1)} %get-tuple-element.43), channel_id=1, source_target_pairs={{0,8},{1,9},{2,10},{3,11},{4,12},{5,13},{6,14},{7,15},{8,0},{9,1},... | collective-permute-start | bytes 307208 | tf_op jit(solution)/shard_map/ppermute | solution.py:351
  19.4 7.1 %collective-permute-start.5 = (f32[5,40,128]{2,1,0:T(8,128)S(1)}, f32[5,40,128]{2,1,0:T(8,128)S(1)}, u32[]{:S(2)}, u32[]{:S(2)}) collective-permute-start(f32[5,40,128]{2,1,0:T(8,128)S(1)} %get-tuple-element.44), channel_id=1, source_target_pairs={{8,16},{9,17},{10,18},{11,19},{12,20},{13,21},{14,22},{15,23},{16,... | collective-permute-start | bytes 307208 | tf_op jit(solution)/shard_map/ppermute | solution.py:352
  27.1 7.8 %collective-permute-start.6 = (f32[112,128]{1,0:T(8,128)S(1)}, f32[112,128]{1,0:T(8,128)S(1)}, u32[]{:S(2)}, u32[]{:S(2)}) collective-permute-start(f32[112,128]{1,0:T(8,128)S(1)} %get-tuple-element.45), channel_id=1, source_target_pairs={{0,1},{1,0},{2,3},{3,2},{4,5},{5,4},{6,7},{7,6},{8,9},{9,8},{10,11... | collective-permute-start | bytes 172040 | tf_op jit(solution)/shard_map/ppermute | solution.py:351
  33.3 1.6 %collective-permute-start.7 = (f32[112,128]{1,0:T(8,128)S(1)}, f32[112,128]{1,0:T(8,128)S(1)}, u32[]{:S(2)}, u32[]{:S(2)}) collective-permute-start(f32[112,128]{1,0:T(8,128)S(1)} %get-tuple-element.46), channel_id=1, source_target_pairs={{1,2},{2,1},{3,4},{4,3},{5,6},{6,5},{9,10},{10,9},{11,12},{12,11},... | collective-permute-start | bytes 172040 | tf_op jit(solution)/shard_map/ppermute | solution.py:352
  39.0 4.9 %collective-permute-start.8 = (f32[5,40,128]{2,1,0:T(8,128)S(1)}, f32[5,40,128]{2,1,0:T(8,128)S(1)}, u32[]{:S(2)}, u32[]{:S(2)}) collective-permute-start(f32[5,40,128]{2,1,0:T(8,128)S(1)} %get-tuple-element.54), channel_id=1, source_target_pairs={{0,8},{1,9},{2,10},{3,11},{4,12},{5,13},{6,14},{7,15},{8,0},{9,1},... | collective-permute-start | bytes 307208 | tf_op jit(solution)/shard_map/ppermute | solution.py:351
  39.1 7.2 %collective-permute-start.9 = (f32[5,40,128]{2,1,0:T(8,128)S(1)}, f32[5,40,128]{2,1,0:T(8,128)S(1)}, u32[]{:S(2)}, u32[]{:S(2)}) collective-permute-start(f32[5,40,128]{2,1,0:T(8,128)S(1)} %get-tuple-element.55), channel_id=1, source_target_pairs={{8,16},{9,17},{10,18},{11,19},{12,20},{13,21},{14,22},{15,23},{16,... | collective-permute-start | bytes 307208 | tf_op jit(solution)/shard_map/ppermute | solution.py:352
  46.9 7.8 %collective-permute-start.10 = (f32[112,128]{1,0:T(8,128)S(1)}, f32[112,128]{1,0:T(8,128)S(1)}, u32[]{:S(2)}, u32[]{:S(2)}) collective-permute-start(f32[112,128]{1,0:T(8,128)S(1)} %get-tuple-element.56), channel_id=1, source_target_pairs={{0,1},{1,0},{2,3},{3,2},{4,5},{5,4},{6,7},{7,6},{8,9},{9,8},{10,11... | collective-permute-start | bytes 172040 | tf_op jit(solution)/shard_map/ppermute | solution.py:351
  53.1 1.6 %collective-permute-start.11 = (f32[112,128]{1,0:T(8,128)S(1)}, f32[112,128]{1,0:T(8,128)S(1)}, u32[]{:S(2)}, u32[]{:S(2)}) collective-permute-start(f32[112,128]{1,0:T(8,128)S(1)} %get-tuple-element.57), channel_id=1, source_target_pairs={{1,2},{2,1},{3,4},{4,3},{5,6},{6,5},{9,10},{10,9},{11,12},{12,11},... | collective-permute-start | bytes 172040 | tf_op jit(solution)/shard_map/ppermute | solution.py:352
  58.8 5.0 %collective-permute-start.12 = (f32[5,40,128]{2,1,0:T(8,128)S(1)}, f32[5,40,128]{2,1,0:T(8,128)S(1)}, u32[]{:S(2)}, u32[]{:S(2)}) collective-permute-start(f32[5,40,128]{2,1,0:T(8,128)S(1)} %get-tuple-element.60), channel_id=1, source_target_pairs={{0,8},{1,9},{2,10},{3,11},{4,12},{5,13},{6,14},{7,15},{8,0},{9,1},... | collective-permute-start | bytes 307208 | tf_op jit(solution)/shard_map/ppermute | solution.py:351
  58.9 7.2 %collective-permute-start.13 = (f32[5,40,128]{2,1,0:T(8,128)S(1)}, f32[5,40,128]{2,1,0:T(8,128)S(1)}, u32[]{:S(2)}, u32[]{:S(2)}) collective-permute-start(f32[5,40,128]{2,1,0:T(8,128)S(1)} %get-tuple-element.61), channel_id=1, source_target_pairs={{8,16},{9,17},{10,18},{11,19},{12,20},{13,21},{14,22},{15,23},{16,... | collective-permute-start | bytes 307208 | tf_op jit(solution)/shard_map/ppermute | solution.py:352
  66.7 10.4 %collective-permute-start.14 = (f32[112,128]{1,0:T(8,128)S(1)}, f32[112,128]{1,0:T(8,128)S(1)}, u32[]{:S(2)}, u32[]{:S(2)}) collective-permute-start(f32[112,128]{1,0:T(8,128)S(1)} %get-tuple-element.62), channel_id=1, source_target_pairs={{0,1},{1,0},{2,3},{3,2},{4,5},{5,4},{6,7},{7,6},{8,9},{9,8},{10,11... | collective-permute-start | bytes 172040 | tf_op jit(solution)/shard_map/ppermute | solution.py:351
  75.5 1.6 %collective-permute-start.15 = (f32[112,128]{1,0:T(8,128)S(1)}, f32[112,128]{1,0:T(8,128)S(1)}, u32[]{:S(2)}, u32[]{:S(2)}) collective-permute-start(f32[112,128]{1,0:T(8,128)S(1)} %get-tuple-element.63), channel_id=1, source_target_pairs={{1,2},{2,1},{3,4},{4,3},{5,6},{6,5},{9,10},{10,9},{11,12},{12,11},... | collective-permute-start | bytes 172040 | tf_op jit(solution)/shard_map/ppermute | solution.py:352
